TPU v7x, 256 devices: a whole 4x4x8 slice. The times are simulated.
256 devices in a mesh: ta: 32 (over z, y_lo, core), gz: 4 (over x), gy: 2 (over y_hi).
Axes of the slice: x: 4, y: 4 (y_hi: 2, y_lo: 2; y = y_hi * 2 + y_lo), z: 8, core: 2. Of those that a mesh axis runs over, the one named last changes fastest.
Arguments:
- right_side: float32 [256, 32, 32, 128], P('ta', 'gz', 'gy'), may hold values from -12 to 12, as said below
- mass_field: float32 [256, 32, 32, 128], P('ta', 'gz', 'gy'), may hold values from 0.05 to 0.8
Outputs:
- solution: float32 [256, 32, 32, 128], P('ta', 'gz', 'gy')
- residual: float32 [256, 32, 32, 128], P('ta', 'gz', 'gy')
Inputs may be any that keep to these rules, and one draw needn't show every extreme that they name: right_side is twice a field constant on aligned blocks of 8 x 8 x 8 x 8 sites plus site-by-site noise, each part within -4 to 4.
All inputs are finite; a program needn't handle non-finite values.
Results may differ from a plain program's by a relative error of at most 0.0003.
Values sent between devices are 32-bit elements.
A program may use at most 128 MiB of HBM per device.

v0:
```python
import jax
import jax.numpy as jnp
from jax import lax
from jax.experimental import pallas as pl
from jax.experimental.pallas import tpu as pltpu
from jax.sharding import PartitionSpec as P

DAMPING = 0.7
OFF = 8
COPIES = 160
MESH = pl.DeviceIdType.MESH


def lanes(like):
    return lax.broadcasted_iota(jnp.int32, like.shape, like.ndim - 1)


def rows(like):
    return lax.broadcasted_iota(jnp.int32, like.shape, like.ndim - 2)


def roll(x, shift, axis):
    return pltpu.roll(x, shift % x.shape[axis], axis)


def ring(x, shift, axis=0):
    shift %= x.shape[axis]
    return jnp.concatenate([x[-shift:], x[:-shift]], axis=axis)


def even(index, step):
    return jnp.bitwise_and(index, step) == 0


def partner(x, step, axis):
    index = lax.broadcasted_iota(jnp.int32, x.shape, axis)
    return jnp.where(even(index, step), roll(x, -step, axis), roll(x, step, axis))


def spread(x, step, axis):
    index = lax.broadcasted_iota(jnp.int32, x.shape, axis)
    low = even(index, step)
    return jnp.where(low, x, roll(x, step, axis)), jnp.where(low, roll(x, -step, axis), x)


def pack4(a, b, c, d):
    lane = lanes(a)
    return jnp.where(
        even(lane, 2), jnp.where(even(lane, 1), a, b), jnp.where(even(lane, 1), c, d)
    )


def unpack4(x):
    last = x.ndim - 1
    first, second = spread(x, 1, last)
    a, c = spread(first, 2, last)
    b, d = spread(second, 2, last)
    return a, b, c, d


def kernel(
    s_ref, m_ref, sol_ref, res_ref,
    v0, s1, m1, v1, p2, s2, m2, u2, v2, d2_own, d2_in, d3, s3, m3, v3, tmp, send_sem, recv_sem,
):
    ta, gz, gy = lax.axis_index("ta"), lax.axis_index("gz"), lax.axis_index("gy")
    nta, ngz, ngy = lax.axis_size("ta"), lax.axis_size("gz"), lax.axis_size("gy")

    def device(a, b, c):
        return (
            lax.rem(ta + (a + nta), nta),
            lax.rem(gz + (b + ngz), ngz),
            lax.rem(gy + c, ngy),
        )

    barrier = pltpu.get_barrier_semaphore()
    near = [(a, b, c) for a in (0, 1, -1) for b in range(4) for c in range(2)][1:]
    far = [(a, 0, 0) for k in range(2, 6) for a in (k, -k)]
    for offset in near + far:
        pl.semaphore_signal(barrier, inc=1, device_id=device(*offset), device_id_type=MESH)
    pl.semaphore_wait(barrier, len(near) + len(far))

    copies, started = [], []

    def send(src, dst, offset):
        i = len(started)
        copy = pltpu.make_async_remote_copy(
            src_ref=src,
            dst_ref=dst,
            send_sem=send_sem.at[i],
            recv_sem=recv_sem.at[i],
            device_id=device(*offset),
            device_id_type=MESH,
        )
        copies.append(copy)
        started.append(i)
        copy.start()
        return copy

    def arrived(some):
        for copy in some:
            copy.wait_recv()

    t_all, y_all = pl.ds(1, 8), pl.ds(OFF, 16)
    z_all = t_all

    def swap0(slot):
        buf = v0.at[slot]
        return [
            send(buf.at[t_all, z_all, pl.ds(OFF + 15, 1)], buf.at[t_all, z_all, pl.ds(OFF - 1, 1)], (0, 0, 1)),
            send(buf.at[t_all, z_all, pl.ds(OFF, 1)], buf.at[t_all, z_all, pl.ds(OFF + 16, 1)], (0, 0, 1)),
            send(buf.at[8, z_all, y_all], buf.at[0, z_all, y_all], (1, 0, 0)),
            send(buf.at[1, z_all, y_all], buf.at[9, z_all, y_all], (-1, 0, 0)),
            send(buf.at[t_all, 8, y_all], buf.at[t_all, 0, y_all], (0, 1, 0)),
            send(buf.at[t_all, 1, y_all], buf.at[t_all, 9, y_all], (0, -1, 0)),
        ]

    def around0(slot, t):
        buf = v0.at[slot]
        mid = buf[t + 1, z_all, y_all, :]
        total = buf[t, z_all, y_all, :] + buf[t + 2, z_all, y_all, :]
        total += buf[t + 1, pl.ds(0, 8), y_all, :] + buf[t + 1, pl.ds(2, 8), y_all, :]
        total += buf[t + 1, z_all, pl.ds(OFF - 1, 16), :] + buf[t + 1, z_all, pl.ds(OFF + 1, 16), :]
        return mid, total + roll(mid, 1, 2) + roll(mid, -1, 2)

    def loop(low, high, body):
        lax.fori_loop(low, high, lambda t, c: (body(t), c)[1], 0)

    def sweep0(slot, out):
        def body(t):
            mid, total = around0(slot, t)
            d = 8.0 + m_ref[t]
            v0[out, t + 1, z_all, y_all, :] = mid + DAMPING * (s_ref[t] - (d * mid - total)) / d

        loop(0, 8, body)

    def residual0(slot, t):
        mid, total = around0(slot, t)
        return s_ref[t] - ((8.0 + m_ref[t]) * mid - total)

    def coarsen_plane(a, step):
        nz, ny, _ = a.shape
        a = a.reshape(nz // 2, 2, ny, 128)
        tmp[0 : nz // 2, 0:ny, :] = a[:, 0] + a[:, 1]
        b = tmp[0 : nz // 2, pl.ds(0, ny // 2, stride=2), :]
        b += tmp[0 : nz // 2, pl.ds(1, ny // 2, stride=2), :]
        return (b + partner(b, step, 2)) * (1.0 / 16.0)

    def swap1(buf, radius):
        def span(k, side):
            if side == 0:
                return pl.ds(3, 4), pl.ds(3, 4)
            if side == 1:
                return pl.ds(7 - k, k), pl.ds(3 - k, k)
            return pl.ds(3, k), pl.ds(7, k)

        group = []
        for a in (0, 1, -1):
            for b in (0, 1, -1):
                for c in (0, 1, -1):
                    k = radius + 1 - abs(a) - abs(b) - abs(c)
                    if k < 1 or not (a or b or c):
                        continue
                    (t_src, t_dst), (z_src, z_dst) = span(k, a), span(k, b)
                    y = {0: pl.ds(0, 8), 1: pl.ds(8 - k, k), -1: pl.ds(0, k)}[c]
                    y_dst = y if c == 0 else pl.ds(y.start + 8, y.size)
                    group.append(
                        send(buf.at[t_src, z_src, y], buf.at[t_dst, z_dst, y_dst], (a, b, abs(c)))
                    )
        return group

    def around1(slot, t, radius):
        nz = 4 + 2 * radius
        z = 3 - radius
        buf = v1.at[slot]
        mid = buf[t, pl.ds(z, nz)]
        total = buf[t - 1, pl.ds(z, nz)] + buf[t + 1, pl.ds(z, nz)]
        total += buf[t, pl.ds(z - 1, nz)] + buf[t, pl.ds(z + 1, nz)]
        total += roll(mid, 1, 1) + roll(mid, -1, 1)
        return mid, total + roll(mid, 2, 2) + roll(mid, -2, 2)

    def sweep1(slot, out, radius):
        z = pl.ds(3 - radius, 4 + 2 * radius)

        def body(t):
            mid, total = around1(slot, t, radius)
            d = 4.0 + m1[t, z]
            v1[out, t, z] = mid + DAMPING * (s1[t, z] - (d * mid - 0.5 * total)) / d

        loop(3 - radius, 7 + radius, body)

    def gather2(buf, block):
        buf[1, 0, 0:4, :] = pack4(block[0, 0], block[0, 1], block[1, 0], block[1, 1])
        own = buf.at[1, 0, pl.ds(0, 4)]
        return [
            send(own, buf.at[1 - a, (4 - b) % 4, pl.ds(4 * c, 4)], (a, b, c)) for a, b, c in near
        ]

    def unpack2(x, into, at):
        a, b, c, d = unpack4(x)
        for z in range(4):
            into[at, 2 * z], into[at, 2 * z + 1] = a[z], b[z]
            into[at + 1, 2 * z], into[at + 1, 2 * z + 1] = c[z], d[z]

    def image(buf, t, level):
        mid = buf[t]
        total = buf[t - 1] + buf[t + 1] + ring(mid, 1) + ring(mid, -1)
        step = level - 1
        total += roll(mid, step, 1) + roll(mid, -step, 1)
        step = 1 << level
        return mid, total + roll(mid, step, 2) + roll(mid, -step, 2)

    def sweep_ring(buf, out, source, mass, low, high, level):
        factor = 0.5**level

        def body(t):
            mid, total = image(buf, t, level)
            d = 8.0 * factor + mass[t]
            out[t] = mid + DAMPING * (source[t] - (d * mid - factor * total)) / d

        loop(low, high, body)

    def coarsen_ring(first, second):
        a = (first + second).reshape(4, 2, 8, 128)
        a = a[:, 0] + a[:, 1]
        a += partner(a, 1, 1)
        return (a + partner(a, 4, 2)) * (1.0 / 16.0)

    def pack3(x):
        row, lane = rows(x[0]), lanes(x[0])
        return jnp.where(
            even(row, 1), jnp.where(even(lane, 1), x[0], x[2]), jnp.where(even(lane, 1), x[1], x[3])
        )

    def unpack3(x, into, t):
        first, second = spread(x, 1, 0)
        into[t, 0], into[t, 2] = spread(first, 1, 1)
        into[t, 1], into[t, 3] = spread(second, 1, 1)

    def first0(t):
        v0[0, t + 1, z_all, y_all, :] = DAMPING * s_ref[t] / (8.0 + m_ref[t])

    loop(0, 8, first0)
    waiting = swap0(0)

    def mass1(t):
        m1[t + 3, pl.ds(3, 4), 0:8, :] = coarsen_plane(m_ref[2 * t] + m_ref[2 * t + 1], 1)

    loop(0, 4, mass1)
    own1 = pl.ds(3, 4)
    for t in range(2):
        s2[4 + t, 0:2, 0:4, :] = coarsen_plane(
            m1[3 + 2 * t, own1, 0:8, :] + m1[4 + 2 * t, own1, 0:8, :], 2
        )
    mass2_in = gather2(p2.at[0], s2[4:6, 0:2, 0:4, :])
    mass1_in = swap1(m1, 2)

    arrived(waiting)
    sweep0(0, 1)
    arrived(swap0(1))

    def down0(t):
        a = residual0(1, 2 * t) + residual0(1, 2 * t + 1)
        s1[t + 3, own1, 0:8, :] = coarsen_plane(a, 1)

    loop(0, 4, down0)
    waiting = swap1(s1, 2)
    arrived(mass1_in)
    arrived(mass2_in)
    for t in range(3):
        unpack2(p2[0, t], m2, 2 + 2 * t)
    d2_own[1] = p2[0, 1]
    mass3 = coarsen_ring(m2[4], m2[5])
    arrived(waiting)

    z_two = pl.ds(1, 8)

    def first1(t):
        v1[0, t, z_two] = DAMPING * s1[t, z_two] / (4.0 + m1[t, z_two])

    loop(1, 9, first1)
    sweep1(0, 1, 1)

    residuals = []
    for t in range(4):
        mid, total = around1(1, 3 + t, 0)
        mid, total = mid[:, 0:8], total[:, 0:8]
        d = 4.0 + m1[3 + t, own1, 0:8, :]
        residuals.append(s1[3 + t, own1, 0:8, :] - (d * mid - 0.5 * total))
    for t in range(2):
        s2[4 + t, 0:2, 0:4, :] = coarsen_plane(residuals[2 * t] + residuals[2 * t + 1], 2)
    waiting = gather2(p2.at[1], s2[4:6, 0:2, 0:4, :])
    for t in range(3, 7):
        v1[2, t, own1, 0:8, :] = v1[1, t, own1, 0:8, :]
    halo1_in = swap1(v1.at[2], 3)
    arrived(waiting)
    for t in range(3):
        unpack2(p2[1, t], s2, 2 + 2 * t)

    for t in range(2, 8):
        u2[t] = DAMPING * s2[t] / (2.0 + m2[t])
    sweep_ring(u2, v2, s2, m2, 3, 7, 2)
    remainders = []
    for t in (4, 5):
        mid, total = image(v2, t, 2)
        remainders.append(s2[t] - ((2.0 + m2[t]) * mid - 0.25 * total))
    d3[5, 0] = pack3(coarsen_ring(*remainders))
    d3[5, 1] = pack3(mass3)
    waiting = [
        send(d3.at[5], d3.at[5 - a], (a, 0, 0)) for k in range(1, 6) for a in (k, -k)
    ]
    d2_own[0] = p2[1, 1]
    pairs = v2[4:6].reshape(2, 4, 2, 8, 128)
    d2_own[2] = pack4(pairs[0, :, 0], pairs[0, :, 1], pairs[1, :, 0], pairs[1, :, 1])
    halo2_in = [
        send(d2_own, d2_in.at[2 - a], (a, 0, 0)) for a in (1, -1, 2, -2)
    ]
    arrived(waiting)

    for t in range(11):
        unpack3(d3[t, 0], s3, t)
        unpack3(d3[t, 1], m3, t)
        v3[0, t] = DAMPING * s3[t] / (1.0 + m3[t])
    for step in range(3):
        sweep_ring(v3.at[step], v3.at[step + 1], s3, m3, 1 + step, 10 - step, 3)

    arrived(halo2_in)
    for k, at in ((0, 0), (1, 2), (3, 6), (4, 8)):
        if k in (0, 4):
            unpack2(d2_in[k, 0], s2, at)
            unpack2(d2_in[k, 1], m2, at)
        unpack2(d2_in[k, 2], v2, at)
    for t in range(10):
        e = v3[3, 3 + t // 2]
        e = jnp.broadcast_to(e[:, None], (4, 2, 8, 128)).reshape(8, 8, 128)
        v2[t] = v2[t] + e
    sweep_ring(v2, u2, s2, m2, 1, 9, 2)
    sweep_ring(u2, v2, s2, m2, 2, 8, 2)

    arrived(halo1_in)
    for copy in halo1_in:
        copy.wait_send()
    copies = [copy for copy in copies if not any(copy is old for old in halo1_in)]
    for tc in range(6):
        for z in range(6):
            e = v2[2 + tc, (z - 2) % 8]
            tmp[z, pl.ds(0, 8, stride=2), :] = e
            tmp[z, pl.ds(1, 8, stride=2), :] = e
        e = tmp[0:6, 0:16, :]
        e = jnp.broadcast_to(e[:, None], (6, 2, 16, 128)).reshape(12, 16, 128)[1:11]
        for k in range(2):
            t = 2 * (tc - 2) + k + 3
            if 0 <= t < 10:
                v1[2, t] = v1[2, t] + e
    sweep1(2, 3, 2)
    sweep1(3, 4, 1)

    for tc in range(6):
        e = v1[4, 2 + tc, pl.ds(2, 6)]
        tmp[0:6, pl.ds(OFF, 8, stride=2), :] = e[:, 0:8]
        tmp[0:6, pl.ds(OFF + 1, 8, stride=2), :] = e[:, 0:8]
        tmp[0:6, OFF - 1 : OFF, :] = e[:, 15:16]
        tmp[0:6, OFF + 16 : OFF + 17, :] = e[:, 8:9]
        e = tmp[...]
        e = jnp.broadcast_to(e[:, None], (6, 2, 32, 128)).reshape(12, 32, 128)[1:11]
        for k in range(2):
            t = 2 * (tc - 1) + k + 1
            if 0 <= t < 10:
                v0[2, t] = v0[1, t] + e
    sweep0(2, 3)
    arrived(swap0(3))
    sweep0(3, 4)
    arrived(swap0(4))

    def finish(t):
        res_ref[t] = residual0(4, t)
        sol_ref[t] = v0[4, t + 1, z_all, y_all, :]

    loop(0, 8, finish)
    for copy in copies:
        copy.wait_send()


def per_device(right_side, mass_field):
    f32 = jnp.float32
    block = jax.ShapeDtypeStruct(right_side.shape, f32)
    vmem = pl.BlockSpec(memory_space=pltpu.VMEM)
    shapes = [
        (5, 10, 10, 32, 128),
        (10, 10, 16, 128), (10, 10, 16, 128), (5, 10, 10, 16, 128),
        (2, 3, 4, 8, 128), (10, 8, 8, 128), (10, 8, 8, 128), (10, 8, 8, 128), (10, 8, 8, 128),
        (3, 4, 8, 128), (5, 3, 4, 8, 128),
        (11, 2, 8, 128), (11, 4, 8, 128), (11, 4, 8, 128), (4, 11, 4, 8, 128),
        (6, 32, 128),
    ]
    scratch = [pltpu.VMEM(shape, f32) for shape in shapes]
    scratch += [pltpu.SemaphoreType.DMA((COPIES,))] * 2
    return pl.pallas_call(
        kernel,
        out_shape=(block, block),
        in_specs=[vmem, vmem],
        out_specs=(vmem, vmem),
        scratch_shapes=scratch,
        compiler_params=pltpu.CompilerParams(
            collective_id=0, has_side_effects=True, vmem_limit_bytes=48 * 1024 * 1024
        ),
    )(right_side, mass_field)


def solution(mesh):
    placed = (P("ta", "gz", "gy", None), P("ta", "gz", "gy", None))
    return jax.shard_map(
        per_device, mesh=mesh, in_specs=placed, out_specs=placed, check_vma=False
    )
```

profile of v0, /device:TPU:1, one launch (start us, length us, event | category | flops | bytes accessed | tf_op | source)
XLA Modules:
  0.0 62.9 jit_solution(13183973955202397252)
XLA Ops:
  0.6 0.0 copy-start
  0.6 1.0 %copy-done = f32[8,8,16,128]{3,2,1,0:T(8,128)S(1)} copy-done((f32[8,8,16,128]{3,2,1,0:T(8,128)S(1)}, f32[8,8,16,128]{3,2,1,0:T(8,128)}, u32[]{:S(2)}) %copy-start) | copy-done | bytes 524312
  1.7 0.0 copy-start.1
  1.7 1.0 %copy-done.1 = f32[8,8,16,128]{3,2,1,0:T(8,128)S(1)} copy-done((f32[8,8,16,128]{3,2,1,0:T(8,128)S(1)}, f32[8,8,16,128]{3,2,1,0:T(8,128)}, u32[]{:S(2)}) %copy-start.1) | copy-done | bytes 524312
  2.7 58.6 %shard_map.41 = (f32[8,8,16,128]{3,2,1,0:T(8,128)S(1)}, f32[8,8,16,128]{3,2,1,0:T(8,128)S(1)}) custom-call(f32[8,8,16,128]{3,2,1,0:T(8,128)S(1)} %copy-done, f32[8,8,16,128]{3,2,1,0:T(8,128)S(1)} %copy-done.1), custom_call_target="tpu_custom_call" | custom-call | tf_op jit(solution)/shard_map/pallas_call | solution.py:397
  61.3 0.8 %copy.6 = f32[8,8,16,128]{3,2,1,0:T(8,128)} copy(f32[8,8,16,128]{3,2,1,0:T(8,128)S(1)} %get-tuple-element.4) | data formatting | bytes 1048576
  62.1 0.8 %copy.7 = f32[8,8,16,128]{3,2,1,0:T(8,128)} copy(f32[8,8,16,128]{3,2,1,0:T(8,128)S(1)} %get-tuple-element.5) | data formatting | bytes 1048576
Async XLA Ops:
  0.6 1.0 %copy-start = (f32[8,8,16,128]{3,2,1,0:T(8,128)S(1)}, f32[8,8,16,128]{3,2,1,0:T(8,128)}, u32[]{:S(2)}) copy-start(f32[8,8,16,128]{3,2,1,0:T(8,128)} %s_ref.1) | copy-start | bytes 1572868
  1.7 1.0 %copy-start.1 = (f32[8,8,16,128]{3,2,1,0:T(8,128)S(1)}, f32[8,8,16,128]{3,2,1,0:T(8,128)}, u32[]{:S(2)}) copy-start(f32[8,8,16,128]{3,2,1,0:T(8,128)} %m_ref.1) | copy-start | bytes 1572868
where the time goes:
time: 63.1 us; the launch traced here: 62.9 us
  Pallas kernels  58.6 us (93%)
  local copies, waits for them, and re-layouts  3.66 us (6%)
  between operations  0.65 us (1%)
    pallas_call x1, Pallas kernels, per_device(): pl.pallas_call(kernel, out_shape=(block, block), in_specs=[vmem, vmem], o...  58.6 us
    unnamed x6, local copies, waits for them, and re-layouts  3.66 us

commit v1 on v0

v1 whole, which is shorter than its diff:
```python
import jax
import jax.numpy as jnp
from jax import lax
from jax.experimental import pallas as pl
from jax.experimental.pallas import tpu as pltpu
from jax.sharding import PartitionSpec as P

DAMPING = 0.7
OFF = 8
ROWS = 8192
MESH = pl.DeviceIdType.MESH


def lanes(like):
    return lax.broadcasted_iota(jnp.int32, like.shape, like.ndim - 1)


def rows(like):
    return lax.broadcasted_iota(jnp.int32, like.shape, like.ndim - 2)


def roll(x, shift, axis):
    return pltpu.roll(x, shift % x.shape[axis], axis)


def ring(x, shift, axis=0):
    shift %= x.shape[axis]
    cut = x.shape[axis] - shift
    return jnp.concatenate(
        [lax.slice_in_dim(x, cut, x.shape[axis], axis=axis), lax.slice_in_dim(x, 0, cut, axis=axis)], axis=axis
    )


def even(index, step):
    return jnp.bitwise_and(index, step) == 0


def partner(x, step, axis):
    index = lax.broadcasted_iota(jnp.int32, x.shape, axis)
    return jnp.where(even(index, step), roll(x, -step, axis), roll(x, step, axis))


def spread(x, step, axis):
    index = lax.broadcasted_iota(jnp.int32, x.shape, axis)
    low = even(index, step)
    return jnp.where(low, x, roll(x, step, axis)), jnp.where(low, roll(x, -step, axis), x)


def pack4(a, b, c, d):
    lane = lanes(a)
    return jnp.where(
        even(lane, 2), jnp.where(even(lane, 1), a, b), jnp.where(even(lane, 1), c, d)
    )


def unpack4(x):
    last = x.ndim - 1
    first, second = spread(x, 1, last)
    a, c = spread(first, 2, last)
    b, d = spread(second, 2, last)
    return a, b, c, d


def kernel(
    s_hbm, m_hbm, sol_ref, res_ref,
    s0, m0, w0, r0, v0, ht, hz, hy, s1, m1, w1, v1, p2, s2, m2, w2, u2, v2, d2_own, d2_in, d3, s3, w3, v3, tmp, bytes_ref,
    load_sem, send_sem, recv_sem,
):
    ta, gz, gy = lax.axis_index("ta"), lax.axis_index("gz"), lax.axis_index("gy")
    nta, ngz, ngy = lax.axis_size("ta"), lax.axis_size("gz"), lax.axis_size("gy")

    load_m = pltpu.make_async_copy(m_hbm, m0, load_sem.at[0])
    load_s = pltpu.make_async_copy(s_hbm, s0, load_sem.at[1])
    load_m.start()
    load_s.start()

    def device(a, b, c):
        return (
            lax.rem(ta + (a + nta), nta),
            lax.rem(gz + (b + ngz), ngz),
            lax.rem(gy + c, ngy),
        )

    barrier = pltpu.get_barrier_semaphore()
    near = [(a, b, c) for a in (0, 1, -1) for b in range(4) for c in range(2)][1:]
    far = [(a, 0, 0) for k in range(2, 6) for a in (k, -k)]
    for offset in near + far:
        pl.semaphore_signal(barrier, inc=1, device_id=device(*offset), device_id_type=MESH)

    groups = []
    sends = [0, 0]

    class Group:
        def __init__(self, sender=0):
            self.number, self.count, self.sender = len(groups), 0, sender
            groups.append(self)

        def send(self, src, dst, offset):
            size = 1
            for extent in dst.shape[:-1]:
                size *= extent
            self.count += size
            sends[self.sender] += size
            pltpu.make_async_remote_copy(
                src_ref=src,
                dst_ref=dst,
                send_sem=send_sem.at[self.sender],
                recv_sem=recv_sem.at[self.number],
                device_id=device(*offset),
                device_id_type=MESH,
            ).start()

        def arrived(self):
            whole = bytes_ref.at[pl.ds(0, self.count)]
            pltpu.make_async_copy(whole, whole, recv_sem.at[self.number]).wait()

    def all_sent(sender):
        whole = bytes_ref.at[pl.ds(0, sends[sender])]
        pltpu.make_async_copy(whole, whole, send_sem.at[sender]).wait()

    def loop(low, high, body):
        lax.fori_loop(low, high, lambda t, c: (body(t), c)[1], 0)

    t_all, y_all = pl.ds(1, 8), pl.ds(OFF, 16)
    z_all = t_all

    def swap0(slot, n):
        buf = v0.at[slot]
        group = Group()
        group.send(buf.at[t_all, 8, y_all], hz.at[n, 0], (0, 1, 0))
        group.send(buf.at[t_all, 1, y_all], hz.at[n, 1], (0, -1, 0))
        one = pl.ds(0, 1)
        whole = pl.ds(0, 8)
        group.send(buf.at[t_all, z_all, pl.ds(OFF + 15, 1)], hy.at[n, 0, whole, whole, one], (0, 0, 1))
        group.send(buf.at[t_all, z_all, pl.ds(OFF, 1)], hy.at[n, 1, whole, whole, pl.ds(7, 1)], (0, 0, 1))
        group.send(buf.at[8, z_all, y_all], ht.at[n, 0], (1, 0, 0))
        group.send(buf.at[1, z_all, y_all], ht.at[n, 1], (-1, 0, 0))
        return group

    def around0(slot, t):
        buf = v0.at[slot]
        mid = buf[t + 1, z_all, y_all, :]
        total = buf[t, z_all, y_all, :] + buf[t + 2, z_all, y_all, :]
        total += buf[t + 1, pl.ds(0, 8), y_all, :] + buf[t + 1, pl.ds(2, 8), y_all, :]
        total += buf[t + 1, z_all, pl.ds(OFF - 1, 16), :] + buf[t + 1, z_all, pl.ds(OFF + 1, 16), :]
        return mid, total + roll(mid, 1, 2) + roll(mid, -1, 2)

    def clear0(slot):
        zero = jnp.zeros((8, 16, 128), jnp.float32)
        v0[slot, 0, z_all, y_all, :] = zero
        v0[slot, 9, z_all, y_all, :] = zero
        rim = jnp.zeros((8, OFF, 128), jnp.float32)

        def body(t):
            v0[slot, t + 1, 0, y_all, :] = zero[0]
            v0[slot, t + 1, 9, y_all, :] = zero[0]
            v0[slot, t + 1, z_all, pl.ds(0, OFF), :] = rim
            v0[slot, t + 1, z_all, pl.ds(OFF + 16, OFF), :] = rim

        loop(0, 8, body)

    def sweep0(slot, out):
        def body(t):
            mid, total = around0(slot, t)
            v0[out, t + 1, z_all, y_all, :] = (1.0 - DAMPING) * mid + v0[0, t + 1, z_all, y_all, :] + w0[t] * total

        loop(0, 8, body)

    def residual0(slot, t):
        mid, total = around0(slot, t)
        return s0[t] - ((8.0 + m0[t]) * mid - total)

    def halo_y(n, t):
        low, high = hy[n, 0, t], hy[n, 1, t]
        low = jnp.where(rows(low) == 0, low, 0.0)
        high = jnp.where(rows(high) == 7, high, 0.0)
        return jnp.concatenate([low, high], axis=1)

    def fix0(out, n):
        def body(t):
            v0[out, t + 1, z_all, y_all, :] = v0[out, t + 1, z_all, y_all, :] + w0[t] * halo_y(n, t)
            for side, z in ((0, 0), (1, 7)):
                v0[out, t + 1, z + 1, y_all, :] = v0[out, t + 1, z + 1, y_all, :] + w0[t, z] * hz[n, side, t]

        loop(0, 8, body)
        for side, t in ((0, 0), (1, 7)):
            v0[out, t + 1, z_all, y_all, :] = v0[out, t + 1, z_all, y_all, :] + w0[t] * ht[n, side]

    def add_halos(ref, n):
        def body(t):
            ref[t] = ref[t] + halo_y(n, t)
            for side, z in ((0, 0), (1, 7)):
                ref[t, z] = ref[t, z] + hz[n, side, t]

        loop(0, 8, body)
        for side, t in ((0, 0), (1, 7)):
            ref[t] = ref[t] + ht[n, side]

    def coarsen_plane(a, step):
        nz, ny, _ = a.shape
        a = a.reshape(nz // 2, 2, ny, 128)
        tmp[0 : nz // 2, 0:ny, :] = a[:, 0] + a[:, 1]
        b = tmp[0 : nz // 2, pl.ds(0, ny // 2, stride=2), :]
        b += tmp[0 : nz // 2, pl.ds(1, ny // 2, stride=2), :]
        return (b + partner(b, step, 2)) * (1.0 / 16.0)

    def swap1(buf, radius, sender=0):
        def span(k, side):
            if side == 0:
                return pl.ds(3, 4), pl.ds(3, 4)
            if side == 1:
                return pl.ds(7 - k, k), pl.ds(3 - k, k)
            return pl.ds(3, k), pl.ds(7, k)

        group = Group(sender)
        offsets = [(a, b, c) for a in (0, 1, -1) for b in (0, 1, -1) for c in (0, 1, -1)][1:]
        for a, b, c in sorted(offsets, key=lambda o: -sum(map(abs, o))):
            k = radius + 1 - abs(a) - abs(b) - abs(c)
            if k < 1:
                continue
            (t_src, t_dst), (z_src, z_dst) = span(k, a), span(k, b)
            y = {0: pl.ds(0, 8), 1: pl.ds(8 - k, k), -1: pl.ds(0, k)}[c]
            y_dst = y if c == 0 else pl.ds(y.start + 8, y.size)
            group.send(buf.at[t_src, z_src, y], buf.at[t_dst, z_dst, y_dst], (a, b, abs(c)))
        return group

    def around1(slot, t, radius):
        nz = 4 + 2 * radius
        z = 3 - radius
        buf = v1.at[slot]
        mid = buf[t, pl.ds(z, nz)]
        total = buf[t - 1, pl.ds(z, nz)] + buf[t + 1, pl.ds(z, nz)]
        total += buf[t, pl.ds(z - 1, nz)] + buf[t, pl.ds(z + 1, nz)]
        total += roll(mid, 1, 1) + roll(mid, -1, 1)
        return mid, total + roll(mid, 2, 2) + roll(mid, -2, 2)

    def sweep1(slot, out, radius):
        z = pl.ds(3 - radius, 4 + 2 * radius)

        def body(t):
            mid, total = around1(slot, t, radius)
            v1[out, t, z] = (1.0 - DAMPING) * mid + v1[0, t, z] + w1[t, z] * total

        loop(3 - radius, 7 + radius, body)

    def gather2(buf, block):
        buf[1, 0, 0:4, :] = pack4(block[0, 0], block[0, 1], block[1, 0], block[1, 1])
        own = buf.at[1, 0, pl.ds(0, 4)]
        group = Group()
        for a, b, c in sorted(near, key=lambda o: -(abs(o[0]) + (0, 1, 2, 1)[o[1]] + 2 * o[2])):
            group.send(own, buf.at[1 - a, (4 - b) % 4, pl.ds(4 * c, 4)], (a, b, c))
        return group

    def unpack2(x, into, at):
        a, b, c, d = unpack4(x)
        into[at] = jnp.stack([a, b], axis=1).reshape(8, 8, 128)
        into[at + 1] = jnp.stack([c, d], axis=1).reshape(8, 8, 128)

    def image(buf, t, count, level):
        mid = buf[pl.ds(t, count)]
        total = buf[pl.ds(t - 1, count)] + buf[pl.ds(t + 1, count)] + ring(mid, 1, 1) + ring(mid, -1, 1)
        step = level - 1
        total += roll(mid, step, 2) + roll(mid, -step, 2)
        step = 1 << level
        return mid, total + roll(mid, step, 3) + roll(mid, -step, 3)

    def sweep_ring(buf, out, first, weight, low, high, level, count):
        def body(i):
            t = low + i * count
            mid, total = image(buf, t, count, level)
            span = pl.ds(t, count)
            out[span] = (1.0 - DAMPING) * mid + first[span] + weight[span] * total

        if high - low == count:
            body(0)
        else:
            loop(0, (high - low) // count, body)

    def coarsen_ring(first, second):
        a = (first + second).reshape(4, 2, 8, 128)
        a = a[:, 0] + a[:, 1]
        a += partner(a, 1, 1)
        return (a + partner(a, 4, 2)) * (1.0 / 16.0)

    def pack3(x):
        row, lane = rows(x[0]), lanes(x[0])
        return jnp.where(
            even(row, 1), jnp.where(even(lane, 1), x[0], x[2]), jnp.where(even(lane, 1), x[1], x[3])
        )

    def unpack3(x):
        first, second = spread(x, 1, 0)
        a, c = spread(first, 1, 1)
        b, d = spread(second, 1, 1)
        return jnp.stack([a, b, c, d])

    load_m.wait()
    load_s.wait()

    def first0(t):
        w = DAMPING / (8.0 + m0[t])
        w0[t] = w
        v0[0, t + 1, z_all, y_all, :] = w * s0[t]

    loop(0, 8, first0)
    pl.semaphore_wait(barrier, len(near) + len(far))
    halos = swap0(0, 0)

    def mass1(t):
        m1[t + 3, pl.ds(3, 4), 0:8, :] = coarsen_plane(m0[2 * t] + m0[2 * t + 1], 1)

    loop(0, 4, mass1)
    own1 = pl.ds(3, 4)
    for t in range(2):
        s2[4 + t, 0:2, 0:4, :] = coarsen_plane(
            m1[3 + 2 * t, own1, 0:8, :] + m1[4 + 2 * t, own1, 0:8, :], 2
        )
    mass2_in = gather2(p2.at[0], s2[4:6, 0:2, 0:4, :])
    mass1_in = swap1(m1, 2)
    for slot in (0, 1, 3, 4):
        clear0(slot)
    sweep0(0, 1)

    halos.arrived()
    fix0(1, 0)
    halos = swap0(1, 1)

    def rest0(t):
        r0[t] = residual0(1, t)

    loop(0, 8, rest0)
    halos.arrived()
    add_halos(r0, 1)

    def down0(t):
        s1[t + 3, own1, 0:8, :] = coarsen_plane(r0[2 * t] + r0[2 * t + 1], 1)

    loop(0, 4, down0)
    source1_in = swap1(s1, 2)
    mass1_in.arrived()
    mass2_in.arrived()
    z_two = pl.ds(1, 8)

    def weight1(t):
        w1[t, z_two] = 0.5 * DAMPING / (4.0 + m1[t, z_two])

    loop(1, 9, weight1)
    loop(0, 3, lambda t: unpack2(p2[0, t], m2, 2 + 2 * t))
    mass3 = coarsen_ring(m2[4], m2[5])
    d3[5, 1] = pack3(mass3)
    d2_own[1] = p2[0, 1]

    def weight2(t):
        w2[t] = 0.25 * DAMPING / (2.0 + m2[t])

    loop(2, 8, weight2)
    source1_in.arrived()

    def first1(t):
        v1[0, t, z_two] = 2.0 * w1[t, z_two] * s1[t, z_two]

    loop(1, 9, first1)
    sweep1(0, 1, 1)

    def down1(t):
        mid, total = around1(1, 3 + t, 0)
        mid, total = mid[:, 0:8], total[:, 0:8]
        d = 4.0 + m1[3 + t, own1, 0:8, :]
        r0[t, 0:4, 0:8, :] = s1[3 + t, own1, 0:8, :] - (d * mid - 0.5 * total)

    loop(0, 4, down1)
    for t in range(2):
        s2[4 + t, 0:2, 0:4, :] = coarsen_plane(r0[2 * t, 0:4, 0:8, :] + r0[2 * t + 1, 0:4, 0:8, :], 2)
    source2_in = gather2(p2.at[1], s2[4:6, 0:2, 0:4, :])
    for t in range(3, 7):
        v1[2, t, own1, 0:8, :] = v1[1, t, own1, 0:8, :]
    halo1_in = swap1(v1.at[2], 3, 1)
    source2_in.arrived()
    loop(0, 3, lambda t: unpack2(p2[1, t], s2, 2 + 2 * t))

    def first2(t):
        u2[t] = 4.0 * w2[t] * s2[t]

    loop(2, 8, first2)
    sweep_ring(u2, v2, u2, w2, 3, 7, 2, 4)
    mid, total = image(v2, 4, 2, 2)
    remainder = s2[4:6] - ((2.0 + m2[4:6]) * mid - 0.25 * total)
    d3[5, 0] = pack3(coarsen_ring(remainder[0], remainder[1]))
    planes_in = Group()
    for k in range(5, 0, -1):
        for a in (k, -k):
            planes_in.send(d3.at[5], d3.at[5 - a], (a, 0, 0))
    d2_own[0] = p2[1, 1]
    pairs = v2[4:6].reshape(2, 4, 2, 8, 128)
    d2_own[2] = pack4(pairs[0, :, 0], pairs[0, :, 1], pairs[1, :, 0], pairs[1, :, 1])
    halo2_in = Group()
    for a in (1, -1, 2, -2):
        halo2_in.send(d2_own, d2_in.at[2 - a], (a, 0, 0))
    planes_in.arrived()

    def first3(t):
        w = 0.125 * DAMPING / (1.0 + unpack3(d3[t, 1]))
        w3[t] = w
        v3[0, t] = 8.0 * w * unpack3(d3[t, 0])

    loop(0, 11, first3)
    for step in range(3):
        sweep_ring(v3.at[step], v3.at[step + 1], v3.at[0], w3, 1 + step, 10 - step, 3, 9 - 2 * step)

    halo2_in.arrived()
    for k, at in ((0, 0), (4, 8)):
        unpack2(d2_in[k, 0], s2, at)
        unpack2(d2_in[k, 1], m2, at)
    for k, at in ((0, 0), (1, 2), (3, 6), (4, 8)):
        unpack2(d2_in[k, 2], v2, at)
    for at in (0, 8):
        w = 0.25 * DAMPING / (2.0 + m2[at : at + 2])
        w2[at : at + 2] = w
        u2[at : at + 2] = 4.0 * w * s2[at : at + 2]

    def correct2(t):
        e = v3[3, 3 + t]
        e = jnp.broadcast_to(e[:, None], (4, 2, 8, 128)).reshape(8, 8, 128)
        for k in range(2):
            v2[2 * t + k] = v2[2 * t + k] + e

    loop(0, 5, correct2)
    sweep_ring(v2, s2, u2, w2, 1, 9, 2, 2)
    sweep_ring(s2, v2, u2, w2, 2, 8, 2, 2)

    halo1_in.arrived()
    all_sent(1)

    def expand1(tc):
        for z in range(6):
            e = v2[2 + tc, (z - 2) % 8]
            tmp[z, pl.ds(0, 8, stride=2), :] = e
            tmp[z, pl.ds(1, 8, stride=2), :] = e
        e = tmp[0:6, 0:16, :]
        return jnp.broadcast_to(e[:, None], (6, 2, 16, 128)).reshape(12, 16, 128)[1:11]

    e = expand1(0)
    v1[2, 0] = v1[2, 0] + e

    def correct1(tc):
        e = expand1(tc)
        for k in range(2):
            v1[2, 2 * tc + k - 1] = v1[2, 2 * tc + k - 1] + e

    loop(1, 5, correct1)
    e = expand1(5)
    v1[2, 9] = v1[2, 9] + e
    sweep1(2, 3, 2)
    sweep1(3, 4, 1)

    def expand0(tc):
        e = v1[4, 2 + tc, pl.ds(2, 6)]
        tmp[0:6, pl.ds(OFF, 8, stride=2), :] = e[:, 0:8]
        tmp[0:6, pl.ds(OFF + 1, 8, stride=2), :] = e[:, 0:8]
        tmp[0:6, OFF - 1 : OFF, :] = e[:, 15:16]
        tmp[0:6, OFF + 16 : OFF + 17, :] = e[:, 8:9]
        e = tmp[...]
        return jnp.broadcast_to(e[:, None], (6, 2, 32, 128)).reshape(12, 32, 128)[1:11]

    v0[2, 0] = expand0(0)

    def correct0(tc):
        e = expand0(tc)
        for k in range(2):
            v0[2, 2 * tc + k - 1] = v0[1, 2 * tc + k - 1] + e

    loop(1, 5, correct0)
    v0[2, 9] = expand0(5)
    sweep0(2, 3)
    fix0(3, 1)
    halos = swap0(3, 2)
    sweep0(3, 4)
    halos.arrived()
    fix0(4, 2)
    halos = swap0(4, 3)

    def finish(t):
        res_ref[t] = residual0(4, t)
        sol_ref[t] = v0[4, t + 1, z_all, y_all, :]

    loop(0, 8, finish)
    halos.arrived()
    add_halos(res_ref, 3)
    all_sent(0)


def per_device(right_side, mass_field):
    f32 = jnp.float32
    block = jax.ShapeDtypeStruct(right_side.shape, f32)
    vmem = pl.BlockSpec(memory_space=pltpu.VMEM)
    hbm = pl.BlockSpec(memory_space=pltpu.HBM)
    own, ring2, ring3 = (8, 8, 16, 128), (10, 8, 8, 128), (11, 4, 8, 128)
    shapes = [
        own, own, own, own, (5, 10, 10, 32, 128),
        (4, 2, 8, 16, 128), (4, 2, 8, 16, 128), (4, 2, 8, 8, 8, 128),
        (10, 10, 16, 128), (10, 10, 16, 128), (10, 10, 16, 128), (5, 10, 10, 16, 128),
        (2, 3, 4, 8, 128), ring2, ring2, ring2, ring2, ring2, (3, 4, 8, 128), (5, 3, 4, 8, 128),
        (11, 2, 8, 128), ring3, ring3, (4,) + ring3,
        (6, 32, 128), (ROWS, 128),
    ]
    scratch = [pltpu.VMEM(shape, f32) for shape in shapes]
    scratch += [pltpu.SemaphoreType.DMA((count,)) for count in (2, 2, 11)]
    return pl.pallas_call(
        kernel,
        out_shape=(block, block),
        in_specs=[hbm, hbm],
        out_specs=(vmem, vmem),
        scratch_shapes=scratch,
        compiler_params=pltpu.CompilerParams(
            collective_id=0, has_side_effects=True, vmem_limit_bytes=56 * 1024 * 1024
        ),
    )(right_side, mass_field)


def solution(mesh):
    placed = (P("ta", "gz", "gy", None), P("ta", "gz", "gy", None))
    return jax.shard_map(
        per_device, mesh=mesh, in_specs=placed, out_specs=placed, check_vma=False
    )
```

time: 63.1 us -> 56.2 us (0.89)
  Pallas kernels: 58.6 us -> 52.7 us
  local copies, waits for them, and re-layouts: 3.66 us -> 2.72 us
    pallas_call x1, Pallas kernels: 58.6 us -> 52.7 us  [per_device(): pl.pallas_call(kernel, out_shape=(block, block), in_specs=[hbm, hbm], out...]
    unnamed x6 -> x4, local copies, waits for them, and re-layouts: 3.66 us -> 2.72 us
where the time goes in v1:
time: 56.2 us; the launch traced here: 56.1 us
  Pallas kernels  52.7 us (94%)
  local copies, waits for them, and re-layouts  2.72 us (5%)
  between operations  0.65 us (1%)
    pallas_call x1, Pallas kernels, per_device(): pl.pallas_call(kernel, out_shape=(block, block), in_specs=[hbm, hbm], out...  52.7 us
    unnamed x4, local copies, waits for them, and re-layouts  2.72 us

profile of v1, /device:TPU:1, one launch (start us, length us, event | category | flops | bytes accessed | tf_op | source)
XLA Modules:
  0.0 56.1 jit_solution(8413036866995434225)
XLA Ops:
  0.6 52.7 %shard_map.41 = (f32[8,8,16,128]{3,2,1,0:T(8,128)}, f32[8,8,16,128]{3,2,1,0:T(8,128)}) custom-call(f32[8,8,16,128]{3,2,1,0:T(8,128)} %s_hbm.1, f32[8,8,16,128]{3,2,1,0:T(8,128)} %m_hbm.1), custom_call_target="tpu_custom_call" | custom-call | tf_op jit(solution)/shard_map/pallas_call | solution.py:508
  53.3 0.0 copy-start
  53.3 1.9 %copy.6 = f32[8,8,16,128]{3,2,1,0:T(8,128)} copy(f32[8,8,16,128]{3,2,1,0:T(8,128)} %get-tuple-element.4) | data formatting | bytes 1048576
  55.3 0.0 copy-done
  55.3 0.8 %copy.7 = f32[8,8,16,128]{3,2,1,0:T(8,128)} copy(f32[8,8,16,128]{3,2,1,0:T(8,128)S(1)} %copy-done) | data formatting | bytes 1048576
Async XLA Ops:
  53.3 1.9 %copy-start = (f32[8,8,16,128]{3,2,1,0:T(8,128)S(1)}, f32[8,8,16,128]{3,2,1,0:T(8,128)}, u32[]{:S(2)}) copy-start(f32[8,8,16,128]{3,2,1,0:T(8,128)} %get-tuple-element.5) | copy-start | bytes 1572868

commit v2 on v1

--- a/solution.py
+++ b/solution.py
@@ -83,8 +83,8 @@
 
     barrier = pltpu.get_barrier_semaphore()
     near = [(a, b, c) for a in (0, 1, -1) for b in range(4) for c in range(2)][1:]
-    far = [(a, 0, 0) for k in range(2, 6) for a in (k, -k)]
-    for offset in near + far:
+    faces = [(1, 0, 0), (-1, 0, 0), (0, 1, 0), (0, -1, 0), (0, 0, 1)]
+    for offset in faces:
         pl.semaphore_signal(barrier, inc=1, device_id=device(*offset), device_id_type=MESH)
 
     groups = []
@@ -243,12 +243,15 @@
 
         loop(3 - radius, 7 + radius, body)
 
-    def gather2(buf, block):
-        buf[1, 0, 0:4, :] = pack4(block[0, 0], block[0, 1], block[1, 0], block[1, 1])
-        own = buf.at[1, 0, pl.ds(0, 4)]
+    def pack2(kind, block):
+        p2[1, 0, kind, 0:4, :] = pack4(block[0, 0], block[0, 1], block[1, 0], block[1, 1])
+
+    def gather2():
+        whole = pl.ds(0, 2)
+        own = p2.at[1, 0, whole, pl.ds(0, 4)]
         group = Group()
         for a, b, c in sorted(near, key=lambda o: -(abs(o[0]) + (0, 1, 2, 1)[o[1]] + 2 * o[2])):
-            group.send(own, buf.at[1 - a, (4 - b) % 4, pl.ds(4 * c, 4)], (a, b, c))
+            group.send(own, p2.at[1 - a, (4 - b) % 4, whole, pl.ds(4 * c, 4)], (a, b, c))
         return group
 
     def unpack2(x, into, at):
@@ -303,7 +306,7 @@
         v0[0, t + 1, z_all, y_all, :] = w * s0[t]
 
     loop(0, 8, first0)
-    pl.semaphore_wait(barrier, len(near) + len(far))
+    pl.semaphore_wait(barrier, len(faces))
     halos = swap0(0, 0)
 
     def mass1(t):
@@ -315,8 +318,7 @@
         s2[4 + t, 0:2, 0:4, :] = coarsen_plane(
             m1[3 + 2 * t, own1, 0:8, :] + m1[4 + 2 * t, own1, 0:8, :], 2
         )
-    mass2_in = gather2(p2.at[0], s2[4:6, 0:2, 0:4, :])
-    mass1_in = swap1(m1, 2)
+    pack2(1, s2[4:6, 0:2, 0:4, :])
     for slot in (0, 1, 3, 4):
         clear0(slot)
     sweep0(0, 1)
@@ -324,6 +326,7 @@
     halos.arrived()
     fix0(1, 0)
     halos = swap0(1, 1)
+    mass1_in = swap1(m1, 2)
 
     def rest0(t):
         r0[t] = residual0(1, t)
@@ -338,22 +341,12 @@
     loop(0, 4, down0)
     source1_in = swap1(s1, 2)
     mass1_in.arrived()
-    mass2_in.arrived()
     z_two = pl.ds(1, 8)
 
     def weight1(t):
         w1[t, z_two] = 0.5 * DAMPING / (4.0 + m1[t, z_two])
 
     loop(1, 9, weight1)
-    loop(0, 3, lambda t: unpack2(p2[0, t], m2, 2 + 2 * t))
-    mass3 = coarsen_ring(m2[4], m2[5])
-    d3[5, 1] = pack3(mass3)
-    d2_own[1] = p2[0, 1]
-
-    def weight2(t):
-        w2[t] = 0.25 * DAMPING / (2.0 + m2[t])
-
-    loop(2, 8, weight2)
     source1_in.arrived()
 
     def first1(t):
@@ -371,26 +364,33 @@
     loop(0, 4, down1)
     for t in range(2):
         s2[4 + t, 0:2, 0:4, :] = coarsen_plane(r0[2 * t, 0:4, 0:8, :] + r0[2 * t + 1, 0:4, 0:8, :], 2)
-    source2_in = gather2(p2.at[1], s2[4:6, 0:2, 0:4, :])
+    pack2(0, s2[4:6, 0:2, 0:4, :])
+    source2_in = gather2()
     for t in range(3, 7):
         v1[2, t, own1, 0:8, :] = v1[1, t, own1, 0:8, :]
     halo1_in = swap1(v1.at[2], 3, 1)
     source2_in.arrived()
-    loop(0, 3, lambda t: unpack2(p2[1, t], s2, 2 + 2 * t))
 
     def first2(t):
-        u2[t] = 4.0 * w2[t] * s2[t]
-
-    loop(2, 8, first2)
+        unpack2(p2[t, :, 0], s2, 2 + 2 * t)
+        unpack2(p2[t, :, 1], m2, 2 + 2 * t)
+        span = pl.ds(2 + 2 * t, 2)
+        w = 0.25 * DAMPING / (2.0 + m2[span])
+        w2[span] = w
+        u2[span] = 4.0 * w * s2[span]
+
+    loop(0, 3, first2)
     sweep_ring(u2, v2, u2, w2, 3, 7, 2, 4)
     mid, total = image(v2, 4, 2, 2)
     remainder = s2[4:6] - ((2.0 + m2[4:6]) * mid - 0.25 * total)
     d3[5, 0] = pack3(coarsen_ring(remainder[0], remainder[1]))
+    d3[5, 1] = pack3(coarsen_ring(m2[4], m2[5]))
     planes_in = Group()
     for k in range(5, 0, -1):
         for a in (k, -k):
             planes_in.send(d3.at[5], d3.at[5 - a], (a, 0, 0))
-    d2_own[0] = p2[1, 1]
+    d2_own[0] = p2[1, :, 0]
+    d2_own[1] = p2[1, :, 1]
     pairs = v2[4:6].reshape(2, 4, 2, 8, 128)
     d2_own[2] = pack4(pairs[0, :, 0], pairs[0, :, 1], pairs[1, :, 0], pairs[1, :, 1])
     halo2_in = Group()
@@ -499,12 +499,12 @@
         own, own, own, own, (5, 10, 10, 32, 128),
         (4, 2, 8, 16, 128), (4, 2, 8, 16, 128), (4, 2, 8, 8, 8, 128),
         (10, 10, 16, 128), (10, 10, 16, 128), (10, 10, 16, 128), (5, 10, 10, 16, 128),
-        (2, 3, 4, 8, 128), ring2, ring2, ring2, ring2, ring2, (3, 4, 8, 128), (5, 3, 4, 8, 128),
+        (3, 4, 2, 8, 128), ring2, ring2, ring2, ring2, ring2, (3, 4, 8, 128), (5, 3, 4, 8, 128),
         (11, 2, 8, 128), ring3, ring3, (4,) + ring3,
         (6, 32, 128), (ROWS, 128),
     ]
     scratch = [pltpu.VMEM(shape, f32) for shape in shapes]
-    scratch += [pltpu.SemaphoreType.DMA((count,)) for count in (2, 2, 11)]
+    scratch += [pltpu.SemaphoreType.DMA((count,)) for count in (2, 2, 10)]
     return pl.pallas_call(
         kernel,
         out_shape=(block, block),

time: 56.2 us -> 54.6 us (0.972)
  Pallas kernels: 52.7 us -> 51.1 us
    pallas_call x1, Pallas kernels: 52.7 us -> 51.1 us  [per_device(): pl.pallas_call(kernel, out_shape=(block, block), in_specs=[hbm, hbm], out...]
where the time goes in v2:
time: 54.6 us; the launch traced here: 54.5 us
  Pallas kernels  51.1 us (94%)
  local copies, waits for them, and re-layouts  2.72 us (5%)
  between operations  0.65 us (1%)
    pallas_call x1, Pallas kernels, per_device(): pl.pallas_call(kernel, out_shape=(block, block), in_specs=[hbm, hbm], out...  51.1 us
    unnamed x4, local copies, waits for them, and re-layouts  2.72 us

profile of v2, /device:TPU:1, one launch (start us, length us, event | category | flops | bytes accessed | tf_op | source)
XLA Modules:
  0.0 54.5 jit_solution(5591296989667353507)
XLA Ops:
  0.6 51.1 %shard_map.41 = (f32[8,8,16,128]{3,2,1,0:T(8,128)}, f32[8,8,16,128]{3,2,1,0:T(8,128)}) custom-call(f32[8,8,16,128]{3,2,1,0:T(8,128)} %s_hbm.1, f32[8,8,16,128]{3,2,1,0:T(8,128)} %m_hbm.1), custom_call_target="tpu_custom_call" | custom-call | tf_op jit(solution)/shard_map/pallas_call | solution.py:508
  51.8 0.0 copy-start
  51.8 1.9 %copy.6 = f32[8,8,16,128]{3,2,1,0:T(8,128)} copy(f32[8,8,16,128]{3,2,1,0:T(8,128)} %get-tuple-element.4) | data formatting | bytes 1048576
  53.7 0.0 copy-done
  53.7 0.8 %copy.7 = f32[8,8,16,128]{3,2,1,0:T(8,128)} copy(f32[8,8,16,128]{3,2,1,0:T(8,128)S(1)} %copy-done) | data formatting | bytes 1048576
Async XLA Ops:
  51.8 1.9 %copy-start = (f32[8,8,16,128]{3,2,1,0:T(8,128)S(1)}, f32[8,8,16,128]{3,2,1,0:T(8,128)}, u32[]{:S(2)}) copy-start(f32[8,8,16,128]{3,2,1,0:T(8,128)} %get-tuple-element.5) | copy-start | bytes 1572868

commit v3 on v2

--- a/solution.py
+++ b/solution.py
@@ -7,6 +7,8 @@
 
 DAMPING = 0.7
 OFF = 8
+GROUP = 2
+GROUP1 = 2
 ROWS = 8192
 MESH = pl.DeviceIdType.MESH
 
@@ -63,12 +65,15 @@
 
 def kernel(
     s_hbm, m_hbm, sol_ref, res_ref,
-    s0, m0, w0, r0, v0, ht, hz, hy, s1, m1, w1, v1, p2, s2, m2, w2, u2, v2, d2_own, d2_in, d3, s3, w3, v3, tmp, bytes_ref,
+    s0, m0, w0, r0, v0_0, v0_1, v0_2, v0_3, v0_4, ht, hz, hy,
+    s1, m1, w1, v1_0, v1_1, v1_2, v1_3, v1_4, p2, s2, m2, w2, u2, v2, d2_own, d2_in, d3, w3, v3_0, v3_1, v3_2, v3_3, tmp, bytes_ref,
     load_sem, send_sem, recv_sem,
 ):
     ta, gz, gy = lax.axis_index("ta"), lax.axis_index("gz"), lax.axis_index("gy")
     nta, ngz, ngy = lax.axis_size("ta"), lax.axis_size("gz"), lax.axis_size("gy")
 
+    v0, v1 = (v0_0, v0_1, v0_2, v0_3, v0_4), (v1_0, v1_1, v1_2, v1_3, v1_4)
+    v3 = (v3_0, v3_1, v3_2, v3_3)
     load_m = pltpu.make_async_copy(m_hbm, m0, load_sem.at[0])
     load_s = pltpu.make_async_copy(s_hbm, s0, load_sem.at[1])
     load_m.start()
@@ -125,7 +130,7 @@
     z_all = t_all
 
     def swap0(slot, n):
-        buf = v0.at[slot]
+        buf = v0[slot]
         group = Group()
         group.send(buf.at[t_all, 8, y_all], hz.at[n, 0], (0, 1, 0))
         group.send(buf.at[t_all, 1, y_all], hz.at[n, 1], (0, -1, 0))
@@ -138,37 +143,41 @@
         return group
 
     def around0(slot, t):
-        buf = v0.at[slot]
-        mid = buf[t + 1, z_all, y_all, :]
-        total = buf[t, z_all, y_all, :] + buf[t + 2, z_all, y_all, :]
-        total += buf[t + 1, pl.ds(0, 8), y_all, :] + buf[t + 1, pl.ds(2, 8), y_all, :]
-        total += buf[t + 1, z_all, pl.ds(OFF - 1, 16), :] + buf[t + 1, z_all, pl.ds(OFF + 1, 16), :]
-        return mid, total + roll(mid, 1, 2) + roll(mid, -1, 2)
+        buf = v0[slot]
+        here = pl.ds(t + 1, GROUP)
+        mid = buf[here, z_all, y_all, :]
+        total = roll(mid, 1, 3) + roll(mid, -1, 3)
+        total += buf[pl.ds(t, GROUP), z_all, y_all, :] + buf[pl.ds(t + 2, GROUP), z_all, y_all, :]
+        total += buf[here, pl.ds(0, 8), y_all, :] + buf[here, pl.ds(2, 8), y_all, :]
+        return mid, total + buf[here, z_all, pl.ds(OFF - 1, 16), :] + buf[here, z_all, pl.ds(OFF + 1, 16), :]
 
     def clear0(slot):
         zero = jnp.zeros((8, 16, 128), jnp.float32)
-        v0[slot, 0, z_all, y_all, :] = zero
-        v0[slot, 9, z_all, y_all, :] = zero
+        v0[slot][0, z_all, y_all, :] = zero
+        v0[slot][9, z_all, y_all, :] = zero
         rim = jnp.zeros((8, OFF, 128), jnp.float32)
 
         def body(t):
-            v0[slot, t + 1, 0, y_all, :] = zero[0]
-            v0[slot, t + 1, 9, y_all, :] = zero[0]
-            v0[slot, t + 1, z_all, pl.ds(0, OFF), :] = rim
-            v0[slot, t + 1, z_all, pl.ds(OFF + 16, OFF), :] = rim
+            v0[slot][t + 1, 0, y_all, :] = zero[0]
+            v0[slot][t + 1, 9, y_all, :] = zero[0]
+            v0[slot][t + 1, z_all, pl.ds(0, OFF), :] = rim
+            v0[slot][t + 1, z_all, pl.ds(OFF + 16, OFF), :] = rim
 
         loop(0, 8, body)
 
     def sweep0(slot, out):
-        def body(t):
+        def body(i):
+            t = i * GROUP
             mid, total = around0(slot, t)
-            v0[out, t + 1, z_all, y_all, :] = (1.0 - DAMPING) * mid + v0[0, t + 1, z_all, y_all, :] + w0[t] * total
-
-        loop(0, 8, body)
+            here = pl.ds(t + 1, GROUP)
+            old = (1.0 - DAMPING) * mid + v0[0][here, z_all, y_all, :]
+            v0[out][here, z_all, y_all, :] = old + w0[pl.ds(t, GROUP)] * total
+
+        loop(0, 8 // GROUP, body)
 
     def residual0(slot, t):
         mid, total = around0(slot, t)
-        return s0[t] - ((8.0 + m0[t]) * mid - total)
+        return s0[pl.ds(t, GROUP)] - ((8.0 + m0[pl.ds(t, GROUP)]) * mid - total)
 
     def halo_y(n, t):
         low, high = hy[n, 0, t], hy[n, 1, t]
@@ -178,13 +187,13 @@
 
     def fix0(out, n):
         def body(t):
-            v0[out, t + 1, z_all, y_all, :] = v0[out, t + 1, z_all, y_all, :] + w0[t] * halo_y(n, t)
+            v0[out][t + 1, z_all, y_all, :] = v0[out][t + 1, z_all, y_all, :] + w0[t] * halo_y(n, t)
             for side, z in ((0, 0), (1, 7)):
-                v0[out, t + 1, z + 1, y_all, :] = v0[out, t + 1, z + 1, y_all, :] + w0[t, z] * hz[n, side, t]
+                v0[out][t + 1, z + 1, y_all, :] = v0[out][t + 1, z + 1, y_all, :] + w0[t, z] * hz[n, side, t]
 
         loop(0, 8, body)
         for side, t in ((0, 0), (1, 7)):
-            v0[out, t + 1, z_all, y_all, :] = v0[out, t + 1, z_all, y_all, :] + w0[t] * ht[n, side]
+            v0[out][t + 1, z_all, y_all, :] = v0[out][t + 1, z_all, y_all, :] + w0[t] * ht[n, side]
 
     def add_halos(ref, n):
         def body(t):
@@ -224,24 +233,27 @@
             group.send(buf.at[t_src, z_src, y], buf.at[t_dst, z_dst, y_dst], (a, b, abs(c)))
         return group
 
-    def around1(slot, t, radius):
+    def around1(slot, t, count, radius):
         nz = 4 + 2 * radius
         z = 3 - radius
-        buf = v1.at[slot]
-        mid = buf[t, pl.ds(z, nz)]
-        total = buf[t - 1, pl.ds(z, nz)] + buf[t + 1, pl.ds(z, nz)]
-        total += buf[t, pl.ds(z - 1, nz)] + buf[t, pl.ds(z + 1, nz)]
-        total += roll(mid, 1, 1) + roll(mid, -1, 1)
-        return mid, total + roll(mid, 2, 2) + roll(mid, -2, 2)
+        buf = v1[slot]
+        here = pl.ds(t, count)
+        mid = buf[here, pl.ds(z, nz)]
+        total = roll(mid, 2, 3) + roll(mid, -2, 3)
+        total += buf[pl.ds(t - 1, count), pl.ds(z, nz)] + buf[pl.ds(t + 1, count), pl.ds(z, nz)]
+        total += buf[here, pl.ds(z - 1, nz)] + buf[here, pl.ds(z + 1, nz)]
+        return mid, total + roll(mid, 1, 2) + roll(mid, -1, 2)
 
     def sweep1(slot, out, radius):
         z = pl.ds(3 - radius, 4 + 2 * radius)
 
-        def body(t):
-            mid, total = around1(slot, t, radius)
-            v1[out, t, z] = (1.0 - DAMPING) * mid + v1[0, t, z] + w1[t, z] * total
-
-        loop(3 - radius, 7 + radius, body)
+        def body(i):
+            t = 3 - radius + i * GROUP1
+            mid, total = around1(slot, t, GROUP1, radius)
+            here = pl.ds(t, GROUP1)
+            v1[out][here, z] = (1.0 - DAMPING) * mid + v1[0][here, z] + w1[here, z] * total
+
+        loop(0, (4 + 2 * radius) // GROUP1, body)
 
     def pack2(kind, block):
         p2[1, 0, kind, 0:4, :] = pack4(block[0, 0], block[0, 1], block[1, 0], block[1, 1])
@@ -261,11 +273,11 @@
 
     def image(buf, t, count, level):
         mid = buf[pl.ds(t, count)]
-        total = buf[pl.ds(t - 1, count)] + buf[pl.ds(t + 1, count)] + ring(mid, 1, 1) + ring(mid, -1, 1)
+        step = 1 << level
+        total = roll(mid, step, 3) + roll(mid, -step, 3)
+        total += buf[pl.ds(t - 1, count)] + buf[pl.ds(t + 1, count)] + ring(mid, 1, 1) + ring(mid, -1, 1)
         step = level - 1
-        total += roll(mid, step, 2) + roll(mid, -step, 2)
-        step = 1 << level
-        return mid, total + roll(mid, step, 3) + roll(mid, -step, 3)
+        return mid, total + roll(mid, step, 2) + roll(mid, -step, 2)
 
     def sweep_ring(buf, out, first, weight, low, high, level, count):
         def body(i):
@@ -303,7 +315,7 @@
     def first0(t):
         w = DAMPING / (8.0 + m0[t])
         w0[t] = w
-        v0[0, t + 1, z_all, y_all, :] = w * s0[t]
+        v0[0][t + 1, z_all, y_all, :] = w * s0[t]
 
     loop(0, 8, first0)
     pl.semaphore_wait(barrier, len(faces))
@@ -328,10 +340,10 @@
     halos = swap0(1, 1)
     mass1_in = swap1(m1, 2)
 
-    def rest0(t):
-        r0[t] = residual0(1, t)
-
-    loop(0, 8, rest0)
+    def rest0(i):
+        r0[pl.ds(i * GROUP, GROUP)] = residual0(1, i * GROUP)
+
+    loop(0, 8 // GROUP, rest0)
     halos.arrived()
     add_halos(r0, 1)
 
@@ -350,25 +362,22 @@
     source1_in.arrived()
 
     def first1(t):
-        v1[0, t, z_two] = 2.0 * w1[t, z_two] * s1[t, z_two]
+        v1[0][t, z_two] = 2.0 * w1[t, z_two] * s1[t, z_two]
 
     loop(1, 9, first1)
     sweep1(0, 1, 1)
 
-    def down1(t):
-        mid, total = around1(1, 3 + t, 0)
-        mid, total = mid[:, 0:8], total[:, 0:8]
-        d = 4.0 + m1[3 + t, own1, 0:8, :]
-        r0[t, 0:4, 0:8, :] = s1[3 + t, own1, 0:8, :] - (d * mid - 0.5 * total)
-
-    loop(0, 4, down1)
+    mid, total = around1(1, 3, 4, 0)
+    mid, total = mid[:, :, 0:8], total[:, :, 0:8]
+    d = 4.0 + m1[own1, own1, 0:8, :]
+    r0[0:4, 0:4, 0:8, :] = s1[own1, own1, 0:8, :] - (d * mid - 0.5 * total)
     for t in range(2):
         s2[4 + t, 0:2, 0:4, :] = coarsen_plane(r0[2 * t, 0:4, 0:8, :] + r0[2 * t + 1, 0:4, 0:8, :], 2)
     pack2(0, s2[4:6, 0:2, 0:4, :])
     source2_in = gather2()
     for t in range(3, 7):
-        v1[2, t, own1, 0:8, :] = v1[1, t, own1, 0:8, :]
-    halo1_in = swap1(v1.at[2], 3, 1)
+        v1[2][t, own1, 0:8, :] = v1[1][t, own1, 0:8, :]
+    halo1_in = swap1(v1[2], 3, 1)
     source2_in.arrived()
 
     def first2(t):
@@ -401,11 +410,11 @@
     def first3(t):
         w = 0.125 * DAMPING / (1.0 + unpack3(d3[t, 1]))
         w3[t] = w
-        v3[0, t] = 8.0 * w * unpack3(d3[t, 0])
+        v3[0][t] = 8.0 * w * unpack3(d3[t, 0])
 
     loop(0, 11, first3)
     for step in range(3):
-        sweep_ring(v3.at[step], v3.at[step + 1], v3.at[0], w3, 1 + step, 10 - step, 3, 9 - 2 * step)
+        sweep_ring(v3[step], v3[step + 1], v3[0], w3, 1 + step, 10 - step, 3, 9 - 2 * step)
 
     halo2_in.arrived()
     for k, at in ((0, 0), (4, 8)):
@@ -419,14 +428,14 @@
         u2[at : at + 2] = 4.0 * w * s2[at : at + 2]
 
     def correct2(t):
-        e = v3[3, 3 + t]
+        e = v3[3][3 + t]
         e = jnp.broadcast_to(e[:, None], (4, 2, 8, 128)).reshape(8, 8, 128)
         for k in range(2):
             v2[2 * t + k] = v2[2 * t + k] + e
 
     loop(0, 5, correct2)
-    sweep_ring(v2, s2, u2, w2, 1, 9, 2, 2)
-    sweep_ring(s2, v2, u2, w2, 2, 8, 2, 2)
+    sweep_ring(v2, s2, u2, w2, 1, 9, 2, 4)
+    sweep_ring(s2, v2, u2, w2, 2, 8, 2, 3)
 
     halo1_in.arrived()
     all_sent(1)
@@ -440,21 +449,21 @@
         return jnp.broadcast_to(e[:, None], (6, 2, 16, 128)).reshape(12, 16, 128)[1:11]
 
     e = expand1(0)
-    v1[2, 0] = v1[2, 0] + e
+    v1[2][0] = v1[2][0] + e
 
     def correct1(tc):
         e = expand1(tc)
         for k in range(2):
-            v1[2, 2 * tc + k - 1] = v1[2, 2 * tc + k - 1] + e
+            v1[2][2 * tc + k - 1] = v1[2][2 * tc + k - 1] + e
 
     loop(1, 5, correct1)
     e = expand1(5)
-    v1[2, 9] = v1[2, 9] + e
+    v1[2][9] = v1[2][9] + e
     sweep1(2, 3, 2)
     sweep1(3, 4, 1)
 
     def expand0(tc):
-        e = v1[4, 2 + tc, pl.ds(2, 6)]
+        e = v1[4][2 + tc, pl.ds(2, 6)]
         tmp[0:6, pl.ds(OFF, 8, stride=2), :] = e[:, 0:8]
         tmp[0:6, pl.ds(OFF + 1, 8, stride=2), :] = e[:, 0:8]
         tmp[0:6, OFF - 1 : OFF, :] = e[:, 15:16]
@@ -462,15 +471,15 @@
         e = tmp[...]
         return jnp.broadcast_to(e[:, None], (6, 2, 32, 128)).reshape(12, 32, 128)[1:11]
 
-    v0[2, 0] = expand0(0)
+    v0[2][0] = expand0(0)
 
     def correct0(tc):
         e = expand0(tc)
         for k in range(2):
-            v0[2, 2 * tc + k - 1] = v0[1, 2 * tc + k - 1] + e
+            v0[2][2 * tc + k - 1] = v0[1][2 * tc + k - 1] + e
 
     loop(1, 5, correct0)
-    v0[2, 9] = expand0(5)
+    v0[2][9] = expand0(5)
     sweep0(2, 3)
     fix0(3, 1)
     halos = swap0(3, 2)
@@ -479,11 +488,12 @@
     fix0(4, 2)
     halos = swap0(4, 3)
 
-    def finish(t):
-        res_ref[t] = residual0(4, t)
-        sol_ref[t] = v0[4, t + 1, z_all, y_all, :]
-
-    loop(0, 8, finish)
+    def finish(i):
+        here = pl.ds(i * GROUP, GROUP)
+        res_ref[here] = residual0(4, i * GROUP)
+        sol_ref[here] = v0[4][pl.ds(i * GROUP + 1, GROUP), z_all, y_all, :]
+
+    loop(0, 8 // GROUP, finish)
     halos.arrived()
     add_halos(res_ref, 3)
     all_sent(0)
@@ -496,11 +506,11 @@
     hbm = pl.BlockSpec(memory_space=pltpu.HBM)
     own, ring2, ring3 = (8, 8, 16, 128), (10, 8, 8, 128), (11, 4, 8, 128)
     shapes = [
-        own, own, own, own, (5, 10, 10, 32, 128),
+        own, own, own, own, *[(10, 10, 32, 128)] * 5,
         (4, 2, 8, 16, 128), (4, 2, 8, 16, 128), (4, 2, 8, 8, 8, 128),
-        (10, 10, 16, 128), (10, 10, 16, 128), (10, 10, 16, 128), (5, 10, 10, 16, 128),
+        *[(10, 10, 16, 128)] * 8,
         (3, 4, 2, 8, 128), ring2, ring2, ring2, ring2, ring2, (3, 4, 8, 128), (5, 3, 4, 8, 128),
-        (11, 2, 8, 128), ring3, ring3, (4,) + ring3,
+        (11, 2, 8, 128), *[ring3] * 5,
         (6, 32, 128), (ROWS, 128),
     ]
     scratch = [pltpu.VMEM(shape, f32) for shape in shapes]

time: 54.6 us -> 53 us (0.971)
  Pallas kernels: 51.1 us -> 49.5 us
    pallas_call x1, Pallas kernels: 51.1 us -> 49.5 us  [per_device(): pl.pallas_call(kernel, out_shape=(block, block), in_specs=[hbm, hbm], out...]
where the time goes in v3:
time: 53 us; the launch traced here: 52.9 us
  Pallas kernels  49.5 us (93%)
  local copies, waits for them, and re-layouts  2.72 us (5%)
  between operations  0.65 us (1%)
    pallas_call x1, Pallas kernels, per_device(): pl.pallas_call(kernel, out_shape=(block, block), in_specs=[hbm, hbm], out...  49.5 us
    unnamed x4, local copies, waits for them, and re-layouts  2.72 us

profile of v3, /device:TPU:1, one launch (start us, length us, event | category | flops | bytes accessed | tf_op | source)
XLA Modules:
  0.0 52.9 jit_solution(10338240419779934591)
XLA Ops:
  0.6 49.5 %shard_map.41 = (f32[8,8,16,128]{3,2,1,0:T(8,128)}, f32[8,8,16,128]{3,2,1,0:T(8,128)}) custom-call(f32[8,8,16,128]{3,2,1,0:T(8,128)} %s_hbm.1, f32[8,8,16,128]{3,2,1,0:T(8,128)} %m_hbm.1), custom_call_target="tpu_custom_call" | custom-call | tf_op jit(solution)/shard_map/pallas_call | solution.py:518
  50.2 0.0 copy-start
  50.2 1.9 %copy.6 = f32[8,8,16,128]{3,2,1,0:T(8,128)} copy(f32[8,8,16,128]{3,2,1,0:T(8,128)} %get-tuple-element.4) | data formatting | bytes 1048576
  52.1 0.0 copy-done
  52.1 0.8 %copy.7 = f32[8,8,16,128]{3,2,1,0:T(8,128)} copy(f32[8,8,16,128]{3,2,1,0:T(8,128)S(1)} %copy-done) | data formatting | bytes 1048576
Async XLA Ops:
  50.2 1.9 %copy-start = (f32[8,8,16,128]{3,2,1,0:T(8,128)S(1)}, f32[8,8,16,128]{3,2,1,0:T(8,128)}, u32[]{:S(2)}) copy-start(f32[8,8,16,128]{3,2,1,0:T(8,128)} %get-tuple-element.5) | copy-start | bytes 1572868

commit v4 on v3

--- a/solution.py
+++ b/solution.py
@@ -66,7 +66,7 @@
 def kernel(
     s_hbm, m_hbm, sol_ref, res_ref,
     s0, m0, w0, r0, v0_0, v0_1, v0_2, v0_3, v0_4, ht, hz, hy,
-    s1, m1, w1, v1_0, v1_1, v1_2, v1_3, v1_4, p2, s2, m2, w2, u2, v2, d2_own, d2_in, d3, w3, v3_0, v3_1, v3_2, v3_3, tmp, bytes_ref,
+    s1, m1, w1, m2_own, v1_0, v1_1, v1_2, v1_3, v1_4, p2, s2, m2, w2, u2, v2, d2_own, d2_in, d3, w3, v3_0, v3_1, v3_2, v3_3, tmp, pairs, bytes_ref,
     load_sem, send_sem, recv_sem,
 ):
     ta, gz, gy = lax.axis_index("ta"), lax.axis_index("gz"), lax.axis_index("gy")
@@ -205,13 +205,15 @@
         for side, t in ((0, 0), (1, 7)):
             ref[t] = ref[t] + ht[n, side]
 
-    def coarsen_plane(a, step):
-        nz, ny, _ = a.shape
-        a = a.reshape(nz // 2, 2, ny, 128)
-        tmp[0 : nz // 2, 0:ny, :] = a[:, 0] + a[:, 1]
-        b = tmp[0 : nz // 2, pl.ds(0, ny // 2, stride=2), :]
-        b += tmp[0 : nz // 2, pl.ds(1, ny // 2, stride=2), :]
-        return (b + partner(b, step, 2)) * (1.0 / 16.0)
+    def coarsen(a, step):
+        nt, nz, ny, _ = a.shape
+        a = a.reshape(nt // 2, 2, nz // 2, 2, ny, 128)
+        a = a[:, 0] + a[:, 1]
+        t, z = slice(0, nt // 2), slice(0, nz // 2)
+        pairs[t, z, 0:ny, :] = a[:, :, 0] + a[:, :, 1]
+        b = pairs[t, z, pl.ds(0, ny // 2, stride=2), :]
+        b += pairs[t, z, pl.ds(1, ny // 2, stride=2), :]
+        return (b + partner(b, step, 3)) * (1.0 / 16.0)
 
     def swap1(buf, radius, sender=0):
         def span(k, side):
@@ -321,16 +323,10 @@
     pl.semaphore_wait(barrier, len(faces))
     halos = swap0(0, 0)
 
-    def mass1(t):
-        m1[t + 3, pl.ds(3, 4), 0:8, :] = coarsen_plane(m0[2 * t] + m0[2 * t + 1], 1)
-
-    loop(0, 4, mass1)
     own1 = pl.ds(3, 4)
-    for t in range(2):
-        s2[4 + t, 0:2, 0:4, :] = coarsen_plane(
-            m1[3 + 2 * t, own1, 0:8, :] + m1[4 + 2 * t, own1, 0:8, :], 2
-        )
-    pack2(1, s2[4:6, 0:2, 0:4, :])
+    m1[own1, own1, 0:8, :] = coarsen(m0[...], 1)
+    m2_own[...] = coarsen(m1[own1, own1, 0:8, :], 2)
+    pack2(1, m2_own[...])
     for slot in (0, 1, 3, 4):
         clear0(slot)
     sweep0(0, 1)
@@ -347,11 +343,10 @@
     halos.arrived()
     add_halos(r0, 1)
 
-    def down0(t):
-        s1[t + 3, own1, 0:8, :] = coarsen_plane(r0[2 * t] + r0[2 * t + 1], 1)
-
-    loop(0, 4, down0)
-    source1_in = swap1(s1, 2)
+    s1[...] = coarsen(r0[...], 1)
+    d1 = 4.0 + m1[own1, own1, 0:8, :]
+    v1[0][own1, own1, 0:8, :] = DAMPING * s1[...] / d1
+    first1_in = swap1(v1[0], 2)
     mass1_in.arrived()
     z_two = pl.ds(1, 8)
 
@@ -359,21 +354,14 @@
         w1[t, z_two] = 0.5 * DAMPING / (4.0 + m1[t, z_two])
 
     loop(1, 9, weight1)
-    source1_in.arrived()
-
-    def first1(t):
-        v1[0][t, z_two] = 2.0 * w1[t, z_two] * s1[t, z_two]
-
-    loop(1, 9, first1)
+    first1_in.arrived()
     sweep1(0, 1, 1)
 
     mid, total = around1(1, 3, 4, 0)
     mid, total = mid[:, :, 0:8], total[:, :, 0:8]
     d = 4.0 + m1[own1, own1, 0:8, :]
-    r0[0:4, 0:4, 0:8, :] = s1[own1, own1, 0:8, :] - (d * mid - 0.5 * total)
-    for t in range(2):
-        s2[4 + t, 0:2, 0:4, :] = coarsen_plane(r0[2 * t, 0:4, 0:8, :] + r0[2 * t + 1, 0:4, 0:8, :], 2)
-    pack2(0, s2[4:6, 0:2, 0:4, :])
+    source2 = coarsen(s1[...] - (d * mid - 0.5 * total), 2)
+    pack2(0, DAMPING * source2 / (2.0 + m2_own[...]))
     source2_in = gather2()
     for t in range(3, 7):
         v1[2][t, own1, 0:8, :] = v1[1][t, own1, 0:8, :]
@@ -381,51 +369,44 @@
     source2_in.arrived()
 
     def first2(t):
-        unpack2(p2[t, :, 0], s2, 2 + 2 * t)
+        unpack2(p2[t, :, 0], u2, 2 + 2 * t)
         unpack2(p2[t, :, 1], m2, 2 + 2 * t)
         span = pl.ds(2 + 2 * t, 2)
-        w = 0.25 * DAMPING / (2.0 + m2[span])
-        w2[span] = w
-        u2[span] = 4.0 * w * s2[span]
-
-    loop(0, 3, first2)
+        w2[span] = 0.25 * DAMPING / (2.0 + m2[span])
+
+    for t in range(3):
+        first2(t)
     sweep_ring(u2, v2, u2, w2, 3, 7, 2, 4)
     mid, total = image(v2, 4, 2, 2)
-    remainder = s2[4:6] - ((2.0 + m2[4:6]) * mid - 0.25 * total)
-    d3[5, 0] = pack3(coarsen_ring(remainder[0], remainder[1]))
-    d3[5, 1] = pack3(coarsen_ring(m2[4], m2[5]))
+    remainder = (2.0 + m2[4:6]) * (u2[4:6] * (1.0 / DAMPING) - mid) + 0.25 * total
+    weight3 = DAMPING / (1.0 + coarsen_ring(m2[4], m2[5]))
+    d3[5, 0] = pack3(weight3 * coarsen_ring(remainder[0], remainder[1]))
+    d3[5, 1] = pack3(0.125 * weight3)
     planes_in = Group()
     for k in range(5, 0, -1):
         for a in (k, -k):
             planes_in.send(d3.at[5], d3.at[5 - a], (a, 0, 0))
     d2_own[0] = p2[1, :, 0]
-    d2_own[1] = p2[1, :, 1]
-    pairs = v2[4:6].reshape(2, 4, 2, 8, 128)
-    d2_own[2] = pack4(pairs[0, :, 0], pairs[0, :, 1], pairs[1, :, 0], pairs[1, :, 1])
+    for k, field in ((1, w2), (2, v2)):
+        halves = field[4:6].reshape(2, 4, 2, 8, 128)
+        d2_own[k] = pack4(halves[0, :, 0], halves[0, :, 1], halves[1, :, 0], halves[1, :, 1])
     halo2_in = Group()
     for a in (1, -1, 2, -2):
         halo2_in.send(d2_own, d2_in.at[2 - a], (a, 0, 0))
+    halo2_in.arrived()
+    for k, at in ((0, 0), (4, 8)):
+        unpack2(d2_in[k, 0], u2, at)
+        unpack2(d2_in[k, 1], w2, at)
+    for k, at in ((0, 0), (1, 2), (3, 6), (4, 8)):
+        unpack2(d2_in[k, 2], v2, at)
+
     planes_in.arrived()
 
-    def first3(t):
-        w = 0.125 * DAMPING / (1.0 + unpack3(d3[t, 1]))
-        w3[t] = w
-        v3[0][t] = 8.0 * w * unpack3(d3[t, 0])
-
-    loop(0, 11, first3)
+    for t in range(11):
+        v3[0][t] = unpack3(d3[t, 0])
+        w3[t] = unpack3(d3[t, 1])
     for step in range(3):
         sweep_ring(v3[step], v3[step + 1], v3[0], w3, 1 + step, 10 - step, 3, 9 - 2 * step)
-
-    halo2_in.arrived()
-    for k, at in ((0, 0), (4, 8)):
-        unpack2(d2_in[k, 0], s2, at)
-        unpack2(d2_in[k, 1], m2, at)
-    for k, at in ((0, 0), (1, 2), (3, 6), (4, 8)):
-        unpack2(d2_in[k, 2], v2, at)
-    for at in (0, 8):
-        w = 0.25 * DAMPING / (2.0 + m2[at : at + 2])
-        w2[at : at + 2] = w
-        u2[at : at + 2] = 4.0 * w * s2[at : at + 2]
 
     def correct2(t):
         e = v3[3][3 + t]
@@ -508,10 +489,10 @@
     shapes = [
         own, own, own, own, *[(10, 10, 32, 128)] * 5,
         (4, 2, 8, 16, 128), (4, 2, 8, 16, 128), (4, 2, 8, 8, 8, 128),
-        *[(10, 10, 16, 128)] * 8,
+        (4, 4, 8, 128), *[(10, 10, 16, 128)] * 2, (2, 2, 4, 128), *[(10, 10, 16, 128)] * 5,
         (3, 4, 2, 8, 128), ring2, ring2, ring2, ring2, ring2, (3, 4, 8, 128), (5, 3, 4, 8, 128),
         (11, 2, 8, 128), *[ring3] * 5,
-        (6, 32, 128), (ROWS, 128),
+        (6, 32, 128), (4, 4, 16, 128), (ROWS, 128),
     ]
     scratch = [pltpu.VMEM(shape, f32) for shape in shapes]
     scratch += [pltpu.SemaphoreType.DMA((count,)) for count in (2, 2, 10)]

time: 53 us -> 51.2 us (0.966)
  Pallas kernels: 49.5 us -> 47.8 us
    pallas_call x1, Pallas kernels: 49.5 us -> 47.8 us  [per_device(): pl.pallas_call(kernel, out_shape=(block, block), in_specs=[hbm, hbm], out...]
where the time goes in v4:
time: 51.2 us; the launch traced here: 51.1 us
  Pallas kernels  47.8 us (93%)
  local copies, waits for them, and re-layouts  2.72 us (5%)
  between operations  0.65 us (1%)
    pallas_call x1, Pallas kernels, per_device(): pl.pallas_call(kernel, out_shape=(block, block), in_specs=[hbm, hbm], out...  47.8 us
    unnamed x4, local copies, waits for them, and re-layouts  2.72 us

profile of v4, /device:TPU:1, one launch (start us, length us, event | category | flops | bytes accessed | tf_op | source)
XLA Modules:
  0.0 51.1 jit_solution(7981655473692255909)
XLA Ops:
  0.6 47.8 %shard_map.41 = (f32[8,8,16,128]{3,2,1,0:T(8,128)}, f32[8,8,16,128]{3,2,1,0:T(8,128)}) custom-call(f32[8,8,16,128]{3,2,1,0:T(8,128)} %s_hbm.1, f32[8,8,16,128]{3,2,1,0:T(8,128)} %m_hbm.1), custom_call_target="tpu_custom_call" | custom-call | tf_op jit(solution)/shard_map/pallas_call | solution.py:499
  48.4 0.0 copy-start
  48.4 1.9 %copy.6 = f32[8,8,16,128]{3,2,1,0:T(8,128)} copy(f32[8,8,16,128]{3,2,1,0:T(8,128)} %get-tuple-element.4) | data formatting | bytes 1048576
  50.3 0.0 copy-done
  50.3 0.8 %copy.7 = f32[8,8,16,128]{3,2,1,0:T(8,128)} copy(f32[8,8,16,128]{3,2,1,0:T(8,128)S(1)} %copy-done) | data formatting | bytes 1048576
Async XLA Ops:
  48.4 1.9 %copy-start = (f32[8,8,16,128]{3,2,1,0:T(8,128)S(1)}, f32[8,8,16,128]{3,2,1,0:T(8,128)}, u32[]{:S(2)}) copy-start(f32[8,8,16,128]{3,2,1,0:T(8,128)} %get-tuple-element.5) | copy-start | bytes 1572868

commit v5 on v4

--- a/solution.py
+++ b/solution.py
@@ -65,8 +65,8 @@
 
 def kernel(
     s_hbm, m_hbm, sol_ref, res_ref,
-    s0, m0, w0, r0, v0_0, v0_1, v0_2, v0_3, v0_4, ht, hz, hy,
-    s1, m1, w1, m2_own, v1_0, v1_1, v1_2, v1_3, v1_4, p2, s2, m2, w2, u2, v2, d2_own, d2_in, d3, w3, v3_0, v3_1, v3_2, v3_3, tmp, pairs, bytes_ref,
+    s0, m0, w0, r0, v0_0, v0_1, v0_2, v0_3, v0_4, ht, hz, hy, wt, wz, wy,
+    s1, m1, w1, weight_1, m2_own, v1_0, v1_1, v1_2, v1_3, v1_4, p2, s2, m2, w2, u2, v2, d2_own, d2_in, d3, w3, v3_0, v3_1, v3_2, v3_3, tmp, pairs, bytes_ref,
     load_sem, send_sem, recv_sem,
 ):
     ta, gz, gy = lax.axis_index("ta"), lax.axis_index("gz"), lax.axis_index("gy")
@@ -93,7 +93,7 @@
         pl.semaphore_signal(barrier, inc=1, device_id=device(*offset), device_id_type=MESH)
 
     groups = []
-    sends = [0, 0]
+    sends = [0, 0, 0]
 
     class Group:
         def __init__(self, sender=0):
@@ -129,17 +129,28 @@
     t_all, y_all = pl.ds(1, 8), pl.ds(OFF, 16)
     z_all = t_all
 
-    def swap0(slot, n):
+    def swap0(slot, n, sender=0):
         buf = v0[slot]
-        group = Group()
+        group = Group(sender)
         group.send(buf.at[t_all, 8, y_all], hz.at[n, 0], (0, 1, 0))
         group.send(buf.at[t_all, 1, y_all], hz.at[n, 1], (0, -1, 0))
         one = pl.ds(0, 1)
         whole = pl.ds(0, 8)
-        group.send(buf.at[t_all, z_all, pl.ds(OFF + 15, 1)], hy.at[n, 0, whole, whole, one], (0, 0, 1))
-        group.send(buf.at[t_all, z_all, pl.ds(OFF, 1)], hy.at[n, 1, whole, whole, pl.ds(7, 1)], (0, 0, 1))
+        group.send(buf.at[t_all, z_all, pl.ds(OFF + 15, 1)], hy.at[n, whole, whole, pl.ds(7, 1)], (0, 0, 1))
+        group.send(buf.at[t_all, z_all, pl.ds(OFF, 1)], hy.at[n, whole, whole, one], (0, 0, 1))
         group.send(buf.at[8, z_all, y_all], ht.at[n, 0], (1, 0, 0))
         group.send(buf.at[1, z_all, y_all], ht.at[n, 1], (-1, 0, 0))
+        return group
+
+    def swap_weights():
+        group = Group()
+        whole = pl.ds(0, 8)
+        group.send(w0.at[whole, 7], wz.at[0], (0, 1, 0))
+        group.send(w0.at[whole, 0], wz.at[1], (0, -1, 0))
+        group.send(w0.at[whole, whole, pl.ds(15, 1)], wy.at[whole, whole, pl.ds(7, 1)], (0, 0, 1))
+        group.send(w0.at[whole, whole, pl.ds(0, 1)], wy.at[whole, whole, pl.ds(0, 1)], (0, 0, 1))
+        group.send(w0.at[7], wt.at[0], (1, 0, 0))
+        group.send(w0.at[0], wt.at[1], (-1, 0, 0))
         return group
 
     def around0(slot, t):
@@ -180,9 +191,9 @@
         return s0[pl.ds(t, GROUP)] - ((8.0 + m0[pl.ds(t, GROUP)]) * mid - total)
 
     def halo_y(n, t):
-        low, high = hy[n, 0, t], hy[n, 1, t]
-        low = jnp.where(rows(low) == 0, low, 0.0)
-        high = jnp.where(rows(high) == 7, high, 0.0)
+        halo = hy[n, t]
+        low = jnp.where(rows(halo) == 0, roll(halo, 1, 1), 0.0)
+        high = jnp.where(rows(halo) == 7, roll(halo, -1, 1), 0.0)
         return jnp.concatenate([low, high], axis=1)
 
     def fix0(out, n):
@@ -215,7 +226,7 @@
         b += pairs[t, z, pl.ds(1, ny // 2, stride=2), :]
         return (b + partner(b, step, 3)) * (1.0 / 16.0)
 
-    def swap1(buf, radius, sender=0):
+    def swap1(buf, into, widths, sender=0):
         def span(k, side):
             if side == 0:
                 return pl.ds(3, 4), pl.ds(3, 4)
@@ -226,13 +237,13 @@
         group = Group(sender)
         offsets = [(a, b, c) for a in (0, 1, -1) for b in (0, 1, -1) for c in (0, 1, -1)][1:]
         for a, b, c in sorted(offsets, key=lambda o: -sum(map(abs, o))):
-            k = radius + 1 - abs(a) - abs(b) - abs(c)
+            k = widths[abs(a) + abs(b) + abs(c) - 1]
             if k < 1:
                 continue
             (t_src, t_dst), (z_src, z_dst) = span(k, a), span(k, b)
             y = {0: pl.ds(0, 8), 1: pl.ds(8 - k, k), -1: pl.ds(0, k)}[c]
             y_dst = y if c == 0 else pl.ds(y.start + 8, y.size)
-            group.send(buf.at[t_src, z_src, y], buf.at[t_dst, z_dst, y_dst], (a, b, abs(c)))
+            group.send(buf.at[t_src, z_src, y], into.at[t_dst, z_dst, y_dst], (a, b, abs(c)))
         return group
 
     def around1(slot, t, count, radius):
@@ -246,14 +257,14 @@
         total += buf[here, pl.ds(z - 1, nz)] + buf[here, pl.ds(z + 1, nz)]
         return mid, total + roll(mid, 1, 2) + roll(mid, -1, 2)
 
-    def sweep1(slot, out, radius):
+    def sweep1(slot, out, radius, first, weight):
         z = pl.ds(3 - radius, 4 + 2 * radius)
 
         def body(i):
             t = 3 - radius + i * GROUP1
             mid, total = around1(slot, t, GROUP1, radius)
             here = pl.ds(t, GROUP1)
-            v1[out][here, z] = (1.0 - DAMPING) * mid + v1[0][here, z] + w1[here, z] * total
+            v1[out][here, z] = (1.0 - DAMPING) * mid + first[here, z] + weight[here, z] * total
 
         loop(0, (4 + 2 * radius) // GROUP1, body)
 
@@ -324,8 +335,9 @@
     halos = swap0(0, 0)
 
     own1 = pl.ds(3, 4)
-    m1[own1, own1, 0:8, :] = coarsen(m0[...], 1)
-    m2_own[...] = coarsen(m1[own1, own1, 0:8, :], 2)
+    m1[...] = coarsen(m0[...], 1)
+    w1[own1, own1, 0:8, :] = 0.5 * DAMPING / (4.0 + m1[...])
+    m2_own[...] = coarsen(m1[...], 2)
     pack2(1, m2_own[...])
     for slot in (0, 1, 3, 4):
         clear0(slot)
@@ -334,7 +346,7 @@
     halos.arrived()
     fix0(1, 0)
     halos = swap0(1, 1)
-    mass1_in = swap1(m1, 2)
+    weights1_in = swap1(w1, w1, (1, 0, 0))
 
     def rest0(i):
         r0[pl.ds(i * GROUP, GROUP)] = residual0(1, i * GROUP)
@@ -344,28 +356,27 @@
     add_halos(r0, 1)
 
     s1[...] = coarsen(r0[...], 1)
-    d1 = 4.0 + m1[own1, own1, 0:8, :]
-    v1[0][own1, own1, 0:8, :] = DAMPING * s1[...] / d1
-    first1_in = swap1(v1[0], 2)
-    mass1_in.arrived()
-    z_two = pl.ds(1, 8)
-
-    def weight1(t):
-        w1[t, z_two] = 0.5 * DAMPING / (4.0 + m1[t, z_two])
-
-    loop(1, 9, weight1)
+    v1[0][own1, own1, 0:8, :] = 2.0 * w1[own1, own1, 0:8, :] * s1[...]
+    first1_in = swap1(v1[0], v1[0], (2, 1, 0))
+    sweep0(1, 3)
+    fix0(3, 1)
+    halos = swap0(3, 2, 2)
+    weights1_in.arrived()
     first1_in.arrived()
-    sweep1(0, 1, 1)
+    sweep1(0, 1, 1, v1[0], w1)
 
     mid, total = around1(1, 3, 4, 0)
-    mid, total = mid[:, :, 0:8], total[:, :, 0:8]
-    d = 4.0 + m1[own1, own1, 0:8, :]
+    mid1, total1 = mid, total = mid[:, :, 0:8], total[:, :, 0:8]
+    d = 4.0 + m1[...]
     source2 = coarsen(s1[...] - (d * mid - 0.5 * total), 2)
     pack2(0, DAMPING * source2 / (2.0 + m2_own[...]))
     source2_in = gather2()
-    for t in range(3, 7):
-        v1[2][t, own1, 0:8, :] = v1[1][t, own1, 0:8, :]
-    halo1_in = swap1(v1[2], 3, 1)
+    v1[3][own1, own1, 0:8, :] = (
+        (1.0 - DAMPING) * mid1 + v1[0][own1, own1, 0:8, :] + w1[own1, own1, 0:8, :] * total1
+    )
+    halo1_in = swap1(v1[3], v1[3], (2, 2, 1), 1)
+    weight_1[own1, own1, 0:8, :] = w1[own1, own1, 0:8, :]
+    weights_in = swap1(w1, weight_1, (2, 2, 1))
     source2_in.arrived()
 
     def first2(t):
@@ -393,6 +404,7 @@
     halo2_in = Group()
     for a in (1, -1, 2, -2):
         halo2_in.send(d2_own, d2_in.at[2 - a], (a, 0, 0))
+    weights0_in = swap_weights()
     halo2_in.arrived()
     for k, at in ((0, 0), (4, 8)):
         unpack2(d2_in[k, 0], u2, at)
@@ -430,18 +442,19 @@
         return jnp.broadcast_to(e[:, None], (6, 2, 16, 128)).reshape(12, 16, 128)[1:11]
 
     e = expand1(0)
-    v1[2][0] = v1[2][0] + e
+    v1[2][0] = e
 
     def correct1(tc):
         e = expand1(tc)
         for k in range(2):
-            v1[2][2 * tc + k - 1] = v1[2][2 * tc + k - 1] + e
+            v1[2][2 * tc + k - 1] = e
 
     loop(1, 5, correct1)
     e = expand1(5)
-    v1[2][9] = v1[2][9] + e
-    sweep1(2, 3, 2)
-    sweep1(3, 4, 1)
+    v1[2][9] = e
+    weights_in.arrived()
+    sweep1(2, 3, 2, v1[3], weight_1)
+    sweep1(3, 4, 1, v1[0], weight_1)
 
     def expand0(tc):
         e = v1[4][2 + tc, pl.ds(2, 6)]
@@ -457,15 +470,48 @@
     def correct0(tc):
         e = expand0(tc)
         for k in range(2):
-            v0[2][2 * tc + k - 1] = v0[1][2 * tc + k - 1] + e
+            v0[2][2 * tc + k - 1] = e
 
     loop(1, 5, correct0)
     v0[2][9] = expand0(5)
-    sweep0(2, 3)
-    fix0(3, 1)
-    halos = swap0(3, 2)
+    halos.arrived()
+    weights0_in.arrived()
+    all_sent(2)
+    keep = 1.0 - DAMPING
+
+    def add0(i):
+        t = i * GROUP
+        mid, total = around0(2, t)
+        here = pl.ds(t + 1, GROUP)
+        v0[3][here, z_all, y_all, :] = v0[3][here, z_all, y_all, :] + keep * mid + w0[pl.ds(t, GROUP)] * total
+
+    loop(0, 8 // GROUP, add0)
+    buf = v0[2]
+    for side, t, inner in ((0, 0, 1), (1, 9, 8)):
+        mid = buf[t, z_all, y_all, :]
+        total = roll(mid, 1, 2) + roll(mid, -1, 2) + mid + buf[inner, z_all, y_all, :]
+        total += buf[t, pl.ds(0, 8), y_all, :] + buf[t, pl.ds(2, 8), y_all, :]
+        total += buf[t, z_all, pl.ds(OFF - 1, 16), :] + buf[t, z_all, pl.ds(OFF + 1, 16), :]
+        ht[2, side] = ht[2, side] + keep * mid + wt[side] * total
+    for side, z, inner in ((0, 0, 1), (1, 9, 8)):
+        mid = buf[t_all, z, y_all, :]
+        total = roll(mid, 1, 2) + roll(mid, -1, 2) + mid + buf[t_all, inner, y_all, :]
+        total += buf[pl.ds(0, 8), z, y_all, :] + buf[pl.ds(2, 8), z, y_all, :]
+        total += buf[t_all, z, pl.ds(OFF - 1, 16), :] + buf[t_all, z, pl.ds(OFF + 1, 16), :]
+        hz[2, side] = hz[2, side] + keep * mid + wz[side] * total
+    own, other = pl.ds(0, 8), pl.ds(8, 8)
+    mid = v1[4][own1, own1, other, :]
+    inner = v1[4][own1, own1, own, :]
+    common = roll(mid, 1, 3) + roll(mid, -1, 3) + 3.0 * mid
+    common += jnp.where(rows(inner) == 0, roll(inner, 1, 2), roll(inner, -1, 2))
+    for a in range(2):
+        for b in range(2):
+            total = common + v1[4][pl.ds(2 + 2 * a, 4), own1, other, :] + v1[4][own1, pl.ds(2 + 2 * b, 4), other, :]
+            for t in range(4):
+                for z in range(4):
+                    at = (2 * t + a, 2 * z + b)
+                    hy[(2,) + at] = hy[(2,) + at] + keep * mid[t, z] + wy[at] * total[t, z]
     sweep0(3, 4)
-    halos.arrived()
     fix0(4, 2)
     halos = swap0(4, 3)
 
@@ -488,14 +534,15 @@
     own, ring2, ring3 = (8, 8, 16, 128), (10, 8, 8, 128), (11, 4, 8, 128)
     shapes = [
         own, own, own, own, *[(10, 10, 32, 128)] * 5,
-        (4, 2, 8, 16, 128), (4, 2, 8, 16, 128), (4, 2, 8, 8, 8, 128),
-        (4, 4, 8, 128), *[(10, 10, 16, 128)] * 2, (2, 2, 4, 128), *[(10, 10, 16, 128)] * 5,
+        (4, 2, 8, 16, 128), (4, 2, 8, 16, 128), (4, 8, 8, 8, 128),
+        (2, 8, 16, 128), (2, 8, 16, 128), (8, 8, 8, 128),
+        *[(4, 4, 8, 128)] * 2, *[(10, 10, 16, 128)] * 2, (2, 2, 4, 128), *[(10, 10, 16, 128)] * 5,
         (3, 4, 2, 8, 128), ring2, ring2, ring2, ring2, ring2, (3, 4, 8, 128), (5, 3, 4, 8, 128),
         (11, 2, 8, 128), *[ring3] * 5,
         (6, 32, 128), (4, 4, 16, 128), (ROWS, 128),
     ]
     scratch = [pltpu.VMEM(shape, f32) for shape in shapes]
-    scratch += [pltpu.SemaphoreType.DMA((count,)) for count in (2, 2, 10)]
+    scratch += [pltpu.SemaphoreType.DMA((count,)) for count in (2, 3, 13)]
     return pl.pallas_call(
         kernel,
         out_shape=(block, block),

time: 51.2 us -> 49.9 us (0.975)
  Pallas kernels: 47.8 us -> 46.4 us
    pallas_call x1, Pallas kernels: 47.8 us -> 46.4 us  [per_device(): pl.pallas_call(kernel, out_shape=(block, block), in_specs=[hbm, hbm], out...]
where the time goes in v5:
time: 49.9 us; the launch traced here: 49.8 us
  Pallas kernels  46.4 us (93%)
  local copies, waits for them, and re-layouts  2.72 us (5%)
  between operations  0.65 us (1%)
    pallas_call x1, Pallas kernels, per_device(): pl.pallas_call(kernel, out_shape=(block, block), in_specs=[hbm, hbm], out...  46.4 us
    unnamed x4, local copies, waits for them, and re-layouts  2.72 us

profile of v5, /device:TPU:1, one launch (start us, length us, event | category | flops | bytes accessed | tf_op | source)
XLA Modules:
  0.0 49.8 jit_solution(5465848994092874147)
XLA Ops:
  0.6 46.4 %shard_map.41 = (f32[8,8,16,128]{3,2,1,0:T(8,128)}, f32[8,8,16,128]{3,2,1,0:T(8,128)}) custom-call(f32[8,8,16,128]{3,2,1,0:T(8,128)} %s_hbm.1, f32[8,8,16,128]{3,2,1,0:T(8,128)} %m_hbm.1), custom_call_target="tpu_custom_call" | custom-call | tf_op jit(solution)/shard_map/pallas_call | solution.py:546
  47.0 0.0 copy-start
  47.1 1.9 %copy.6 = f32[8,8,16,128]{3,2,1,0:T(8,128)} copy(f32[8,8,16,128]{3,2,1,0:T(8,128)} %get-tuple-element.4) | data formatting | bytes 1048576
  49.0 0.0 copy-done
  49.0 0.8 %copy.7 = f32[8,8,16,128]{3,2,1,0:T(8,128)} copy(f32[8,8,16,128]{3,2,1,0:T(8,128)S(1)} %copy-done) | data formatting | bytes 1048576
Async XLA Ops:
  47.0 1.9 %copy-start = (f32[8,8,16,128]{3,2,1,0:T(8,128)S(1)}, f32[8,8,16,128]{3,2,1,0:T(8,128)}, u32[]{:S(2)}) copy-start(f32[8,8,16,128]{3,2,1,0:T(8,128)} %get-tuple-element.5) | copy-start | bytes 1572868

commit v6 on v5

--- a/solution.py
+++ b/solution.py
@@ -279,10 +279,14 @@
             group.send(own, p2.at[1 - a, (4 - b) % 4, whole, pl.ds(4 * c, 4)], (a, b, c))
         return group
 
-    def unpack2(x, into, at):
+    def unpack2(x, first, second):
         a, b, c, d = unpack4(x)
-        into[at] = jnp.stack([a, b], axis=1).reshape(8, 8, 128)
-        into[at + 1] = jnp.stack([c, d], axis=1).reshape(8, 8, 128)
+        first[0][first[1]] = jnp.stack([a, b], axis=1).reshape(8, 8, 128)
+        second[0][second[1]] = jnp.stack([c, d], axis=1).reshape(8, 8, 128)
+
+    def pack_planes(first, second):
+        first, second = first.reshape(4, 2, 8, 128), second.reshape(4, 2, 8, 128)
+        return pack4(first[:, 0], first[:, 1], second[:, 0], second[:, 1])
 
     def image(buf, t, count, level):
         mid = buf[pl.ds(t, count)]
@@ -380,8 +384,8 @@
     source2_in.arrived()
 
     def first2(t):
-        unpack2(p2[t, :, 0], u2, 2 + 2 * t)
-        unpack2(p2[t, :, 1], m2, 2 + 2 * t)
+        unpack2(p2[t, :, 0], (u2, 2 + 2 * t), (u2, 3 + 2 * t))
+        unpack2(p2[t, :, 1], (m2, 2 + 2 * t), (m2, 3 + 2 * t))
         span = pl.ds(2 + 2 * t, 2)
         w2[span] = 0.25 * DAMPING / (2.0 + m2[span])
 
@@ -397,21 +401,13 @@
     for k in range(5, 0, -1):
         for a in (k, -k):
             planes_in.send(d3.at[5], d3.at[5 - a], (a, 0, 0))
-    d2_own[0] = p2[1, :, 0]
-    for k, field in ((1, w2), (2, v2)):
-        halves = field[4:6].reshape(2, 4, 2, 8, 128)
-        d2_own[k] = pack4(halves[0, :, 0], halves[0, :, 1], halves[1, :, 0], halves[1, :, 1])
+    d2_own[0] = pack_planes(u2[5], w2[5])
+    d2_own[1] = pack_planes(v2[4], v2[5])
+    d2_own[2] = pack_planes(u2[4], w2[4])
     halo2_in = Group()
-    for a in (1, -1, 2, -2):
-        halo2_in.send(d2_own, d2_in.at[2 - a], (a, 0, 0))
+    for a, kind, count in ((2, 0, 2), (-2, 1, 2), (1, 1, 1), (-1, 1, 1)):
+        halo2_in.send(d2_own.at[pl.ds(kind, count)], d2_in.at[2 - a, pl.ds(0, count)], (a, 0, 0))
     weights0_in = swap_weights()
-    halo2_in.arrived()
-    for k, at in ((0, 0), (4, 8)):
-        unpack2(d2_in[k, 0], u2, at)
-        unpack2(d2_in[k, 1], w2, at)
-    for k, at in ((0, 0), (1, 2), (3, 6), (4, 8)):
-        unpack2(d2_in[k, 2], v2, at)
-
     planes_in.arrived()
 
     for t in range(11):
@@ -419,6 +415,12 @@
         w3[t] = unpack3(d3[t, 1])
     for step in range(3):
         sweep_ring(v3[step], v3[step + 1], v3[0], w3, 1 + step, 10 - step, 3, 9 - 2 * step)
+
+    halo2_in.arrived()
+    unpack2(d2_in[0, 0], (u2, 1), (w2, 1))
+    unpack2(d2_in[4, 1], (u2, 8), (w2, 8))
+    for k, kind, at in ((0, 1, 0), (1, 0, 2), (3, 0, 6), (4, 0, 8)):
+        unpack2(d2_in[k, kind], (v2, at), (v2, at + 1))
 
     def correct2(t):
         e = v3[3][3 + t]
@@ -526,6 +528,18 @@
     all_sent(0)
 
 
+def store(sol_ref, res_ref, sol_hbm, res_hbm, sem):
+    copies = []
+    for i, (src, dst) in enumerate(((sol_ref, sol_hbm), (res_ref, res_hbm))):
+        for k in range(4):
+            part = pl.ds(2 * k, 2)
+            copies.append(pltpu.make_async_copy(src.at[part], dst.at[part], sem.at[4 * i + k]))
+    for copy in copies:
+        copy.start()
+    for copy in copies:
+        copy.wait()
+
+
 def per_device(right_side, mass_field):
     f32 = jnp.float32
     block = jax.ShapeDtypeStruct(right_side.shape, f32)
@@ -537,13 +551,13 @@
         (4, 2, 8, 16, 128), (4, 2, 8, 16, 128), (4, 8, 8, 8, 128),
         (2, 8, 16, 128), (2, 8, 16, 128), (8, 8, 8, 128),
         *[(4, 4, 8, 128)] * 2, *[(10, 10, 16, 128)] * 2, (2, 2, 4, 128), *[(10, 10, 16, 128)] * 5,
-        (3, 4, 2, 8, 128), ring2, ring2, ring2, ring2, ring2, (3, 4, 8, 128), (5, 3, 4, 8, 128),
+        (3, 4, 2, 8, 128), ring2, ring2, ring2, ring2, ring2, (3, 4, 8, 128), (5, 2, 4, 8, 128),
         (11, 2, 8, 128), *[ring3] * 5,
         (6, 32, 128), (4, 4, 16, 128), (ROWS, 128),
     ]
     scratch = [pltpu.VMEM(shape, f32) for shape in shapes]
     scratch += [pltpu.SemaphoreType.DMA((count,)) for count in (2, 3, 13)]
-    return pl.pallas_call(
+    outs = pl.pallas_call(
         kernel,
         out_shape=(block, block),
         in_specs=[hbm, hbm],
@@ -553,6 +567,13 @@
             collective_id=0, has_side_effects=True, vmem_limit_bytes=56 * 1024 * 1024
         ),
     )(right_side, mass_field)
+    return pl.pallas_call(
+        store,
+        out_shape=(block, block),
+        in_specs=[vmem, vmem],
+        out_specs=(hbm, hbm),
+        scratch_shapes=[pltpu.SemaphoreType.DMA((8,))],
+    )(*outs)
 
 
 def solution(mesh):

time: 49.9 us -> 47.6 us (0.954)
  local copies, waits for them, and re-layouts: 2.72 us -> 0 us
  Pallas kernels: 46.4 us -> 46.9 us
    unnamed x4 -> x0, local copies, waits for them, and re-layouts: 2.72 us -> none
    pallas_call x0 -> x1, Pallas kernels: none -> 2.22 us  [per_device(): pl.pallas_call(store, out_shape=(block, block), in_specs=[vmem, vmem], ou...]
    pallas_call x1, Pallas kernels: 46.4 us -> 44.6 us  [per_device(): pl.pallas_call(kernel, out_shape=(block, block), in_specs=[hbm, hbm], out...]
where the time goes in v6:
time: 47.6 us; the launch traced here: 47.5 us
  Pallas kernels  46.9 us (99%)
  between operations  0.64 us (1%)
    pallas_call x1, Pallas kernels, per_device(): pl.pallas_call(kernel, out_shape=(block, block), in_specs=[hbm, hbm], out...  44.6 us
    pallas_call x1, Pallas kernels, per_device(): pl.pallas_call(store, out_shape=(block, block), in_specs=[vmem, vmem], ou...  2.22 us

profile of v6, /device:TPU:1, one launch (start us, length us, event | category | flops | bytes accessed | tf_op | source)
XLA Modules:
  0.0 47.5 jit_solution(12471911325470800466)
XLA Ops:
  0.6 44.6 %shard_map.41 = (f32[8,8,16,128]{3,2,1,0:T(8,128)}, f32[8,8,16,128]{3,2,1,0:T(8,128)}) custom-call(f32[8,8,16,128]{3,2,1,0:T(8,128)} %s_hbm.1, f32[8,8,16,128]{3,2,1,0:T(8,128)} %m_hbm.1), custom_call_target="tpu_custom_call" | custom-call | tf_op jit(solution)/shard_map/pallas_call | solution.py:560
  45.3 2.2 %shard_map.42 = (f32[8,8,16,128]{3,2,1,0:T(8,128)}, f32[8,8,16,128]{3,2,1,0:T(8,128)}) custom-call(f32[8,8,16,128]{3,2,1,0:T(8,128)} %get-tuple-element.4.sol_ref, f32[8,8,16,128]{3,2,1,0:T(8,128)} %get-tuple-element.5.res_ref), custom_call_target="tpu_custom_call" | custom-call | tf_op jit(solution)/shard_map/pallas_call | solution.py:570

commit v7 on v6

--- a/solution.py
+++ b/solution.py
@@ -7,7 +7,7 @@
 
 DAMPING = 0.7
 OFF = 8
-GROUP = 2
+GROUP = 4
 GROUP1 = 2
 ROWS = 8192
 MESH = pl.DeviceIdType.MESH

time: 47.6 us -> 47.3 us (level)
  no operation moved by 1% of the time
where the time goes in v7:
time: 47.3 us; the launch traced here: 47.2 us
  Pallas kernels  46.5 us (98%)
  between operations  0.64 us (1%)
    pallas_call x1, Pallas kernels, per_device(): pl.pallas_call(kernel, out_shape=(block, block), in_specs=[hbm, hbm], out...  44.3 us
    pallas_call x1, Pallas kernels, per_device(): pl.pallas_call(store, out_shape=(block, block), in_specs=[vmem, vmem], ou...  2.22 us

profile of v7, /device:TPU:1, one launch (start us, length us, event | category | flops | bytes accessed | tf_op | source)
XLA Modules:
  0.0 47.2 jit_solution(4886357697795999402)
XLA Ops:
  0.6 44.3 %shard_map.41 = (f32[8,8,16,128]{3,2,1,0:T(8,128)}, f32[8,8,16,128]{3,2,1,0:T(8,128)}) custom-call(f32[8,8,16,128]{3,2,1,0:T(8,128)} %s_hbm.1, f32[8,8,16,128]{3,2,1,0:T(8,128)} %m_hbm.1), custom_call_target="tpu_custom_call" | custom-call | tf_op jit(solution)/shard_map/pallas_call | solution.py:560
  44.9 2.2 %shard_map.42 = (f32[8,8,16,128]{3,2,1,0:T(8,128)}, f32[8,8,16,128]{3,2,1,0:T(8,128)}) custom-call(f32[8,8,16,128]{3,2,1,0:T(8,128)} %get-tuple-element.4.sol_ref, f32[8,8,16,128]{3,2,1,0:T(8,128)} %get-tuple-element.5.res_ref), custom_call_target="tpu_custom_call" | custom-call | tf_op jit(solution)/shard_map/pallas_call | solution.py:570

commit v8 on v7

--- a/solution.py
+++ b/solution.py
@@ -8,7 +8,6 @@
 DAMPING = 0.7
 OFF = 8
 GROUP = 4
-GROUP1 = 2
 ROWS = 8192
 MESH = pl.DeviceIdType.MESH
 
@@ -260,13 +259,15 @@
     def sweep1(slot, out, radius, first, weight):
         z = pl.ds(3 - radius, 4 + 2 * radius)
 
+        count = 2 + radius
+
         def body(i):
-            t = 3 - radius + i * GROUP1
-            mid, total = around1(slot, t, GROUP1, radius)
-            here = pl.ds(t, GROUP1)
+            t = 3 - radius + i * count
+            mid, total = around1(slot, t, count, radius)
+            here = pl.ds(t, count)
             v1[out][here, z] = (1.0 - DAMPING) * mid + first[here, z] + weight[here, z] * total
 
-        loop(0, (4 + 2 * radius) // GROUP1, body)
+        loop(0, 2, body)
 
     def pack2(kind, block):
         p2[1, 0, kind, 0:4, :] = pack4(block[0, 0], block[0, 1], block[1, 0], block[1, 1])

time: 47.3 us -> 47.1 us (level)
  no operation moved by 1% of the time
where the time goes in v8:
time: 47.1 us; the launch traced here: 47 us
  Pallas kernels  46.3 us (98%)
  between operations  0.64 us (1%)
    pallas_call x1, Pallas kernels, per_device(): pl.pallas_call(kernel, out_shape=(block, block), in_specs=[hbm, hbm], out...  44.1 us
    pallas_call x1, Pallas kernels, per_device(): pl.pallas_call(store, out_shape=(block, block), in_specs=[vmem, vmem], ou...  2.22 us

profile of v8, /device:TPU:1, one launch (start us, length us, event | category | flops | bytes accessed | tf_op | source)
XLA Modules:
  0.0 47.0 jit_solution(7402462163256759503)
XLA Ops:
  0.6 44.1 %shard_map.41 = (f32[8,8,16,128]{3,2,1,0:T(8,128)}, f32[8,8,16,128]{3,2,1,0:T(8,128)}) custom-call(f32[8,8,16,128]{3,2,1,0:T(8,128)} %s_hbm.1, f32[8,8,16,128]{3,2,1,0:T(8,128)} %m_hbm.1), custom_call_target="tpu_custom_call" | custom-call | tf_op jit(solution)/shard_map/pallas_call | solution.py:561
  44.7 2.2 %shard_map.42 = (f32[8,8,16,128]{3,2,1,0:T(8,128)}, f32[8,8,16,128]{3,2,1,0:T(8,128)}) custom-call(f32[8,8,16,128]{3,2,1,0:T(8,128)} %get-tuple-element.4.sol_ref, f32[8,8,16,128]{3,2,1,0:T(8,128)} %get-tuple-element.5.res_ref), custom_call_target="tpu_custom_call" | custom-call | tf_op jit(solution)/shard_map/pallas_call | solution.py:571
